TPU v7x, 256 devices: a whole 4x4x8 slice. The times are simulated.
256 devices in a mesh: row: 32 (over x, z_hi, y), col: 8 (over z_lo, core).
Axes of the slice: x: 4, y: 4, z: 8 (z_hi: 2, z_lo: 4; z = z_hi * 4 + z_lo), core: 2. Of those that a mesh axis runs over, the one named last changes fastest.
Arguments:
- lanczos_now: float32 [1, 256, 1024], P(None, 'row', 'col'), may hold values from -80 to 80, as said below
- lanczos_prev: float32 [1, 256, 1024], P(None, 'row', 'col'), may hold values from -6 to 6
- beta_prev: float32 [1], replicated, may hold values from 0.3 to 1.5
- valence_energy: float32 [256], P('row'), may hold values from -1.5 to -0.5
- conduction_energy: float32 [1024], P('col'), may hold values from 0.5 to 2.5
- valence_panel: float32 [16384, 256], P(('row', 'col')), may hold values from -0.375 to 0.375
- conduction_panel: float32 [16384, 1024], P(('row', 'col')), may hold values from -0.1875 to 0.1875
- screened_coulomb: float32 [16384, 16384], P('row', 'col'), may hold values from -0.046875 to 0.046875
- bare_coulomb: float32 [16384, 16384], P('row', 'col'), may hold values from -0.046875 to 0.046875
Outputs:
- lanczos_next: float32 [1, 256, 1024], P(None, 'row', 'col')
- coefficients: float32 [1, 2], replicated
Inputs may be any that keep to these rules, and one draw needn't show every extreme that they name: `lanczos_now`: real entries; the vectors of a chain are not normalized.
All inputs are finite; a program needn't handle non-finite values.
Results may differ from a plain program's by a relative error of at most 0.0002.
Values sent between devices are 32-bit elements; how exact they have to be, the bound alone decides.
A program may use at most 128 MiB of HBM per device.

v0:
```python
import jax
import jax.numpy as jnp
from jax import lax
from jax.sharding import Mesh
from jax.sharding import PartitionSpec as P

V = 256
C = 1024
COL = ("col_0", "col_1")
ROW = ("row_0", "row_1", "row_2")
ROW_COL = ("row_0", "row_1", "row_2", "col_0", "col_1")


precise = lax.Precision.HIGHEST
epsilon = 1e-06


def copy_for_each(shard, axis):
    copies = jnp.broadcast_to(shard, (lax.axis_size(axis), *shard.shape))
    return lax.all_to_all(copies, axis, split_axis=0, concat_axis=0, tiled=True)


def joined_along(parts, dim):
    dims = list(parts.shape[1:])
    dims[dim] *= parts.shape[0]
    return jnp.moveaxis(parts, 0, dim).reshape(dims)


def gather_directly(shard, axis, dim):
    parts = copy_for_each(shard, axis)
    return joined_along(parts, dim)


def sent_together(arrays, axis, dim, along):
    ends, at = ([], 0)
    for a in arrays[:-1]:
        at += a.shape[along]
        ends.append(at)
    both = jnp.concatenate(arrays, axis=along)
    return tuple(jnp.split(lax.all_gather(both, axis, axis=dim, tiled=True), ends, axis=along))


def split_up(shard, dim, count):
    before, after = (shard.shape[:dim], shard.shape[dim + 1 :])
    return jnp.moveaxis(shard.reshape(*before, count, -1, *after), dim, 0)


def sent_and_summed(shard, axis, dim):
    parts = split_up(shard, dim, lax.axis_size(axis))
    arrived = lax.all_to_all(parts, axis, split_axis=0, concat_axis=0, tiled=True)
    return arrived.sum(axis=0)


def side_by_side(arrays, axis, dim, along):
    columns = [a.reshape(*a.shape[:along], -1) for a in arrays]
    both = jnp.concatenate(columns, axis=along)
    out, at, done = (sent_and_summed(both, axis, dim), 0, [])
    for a, column in zip(arrays, columns):
        piece = out[..., at : at + column.shape[along]]
        done.append(piece.reshape(*piece.shape[:along], *a.shape[along:]))
        at += column.shape[along]
    return tuple(done)


def reduced_to_own(parts, axes, order):
    inside = parts.shape[1:]
    parts = parts.reshape(*(lax.axis_size(a) for a in axes), *inside)
    parts = jnp.moveaxis(parts, order, range(len(axes))).reshape(-1, *inside)
    for k in order:
        parts = lax.psum_scatter(parts, axes[k], scatter_dimension=0, tiled=True)
    return parts[0]


def sum_by_axis(shard, axes, order, dim):
    count = lax.axis_size(axes)
    return reduced_to_own(split_up(shard, dim, count), axes, order)


def one_axis_at_a_time(shard, axes):
    for axis in axes:
        shard = lax.psum(shard, axis)
    return shard


def per_device(
    lanczos_now,
    lanczos_prev,
    beta_prev,
    valence_energy,
    conduction_energy,
    valence_panel,
    conduction_panel,
    screened_coulomb,
    bare_coulomb,
):
    column_points = screened_coulomb.shape[1]
    wider = gather_directly(lanczos_now, COL, 2)
    vectors = lax.all_gather(wider, ROW, axis=1, tiled=True)
    products = jnp.einsum("pv,kvc->pkc", valence_panel, vectors, precision=precise)
    density = jnp.sum(products * conduction_panel[:, None, :], axis=2)
    pair_local = jnp.einsum("pc,kvc->pkv", conduction_panel, vectors, precision=precise)
    every_panel, every_density = sent_together((valence_panel, density), ROW_COL, 0, 1)
    first_point = lax.axis_index(COL) * column_points
    panel = lax.dynamic_slice_in_dim(every_panel, first_point, column_points, 0)
    far_density = lax.dynamic_slice_in_dim(every_density, first_point, column_points, 0)
    pair_terms = (
        jnp.einsum("mkv,nv->mkn", gather_directly(pair_local, COL, 0), panel, precision=precise)
        * screened_coulomb[:, None, :]
    )
    screened = jnp.einsum("mkn,nv->mkv", pair_terms, panel, precision=precise)
    potential = jnp.dot(bare_coulomb, far_density, precision=precise)
    direct_rows, local_potential = side_by_side((screened, potential), COL, 0, 2)
    weighted = local_potential[:, :, None] * conduction_panel[:, None, :]
    bare_term = jnp.einsum("pv,pkc->vkc", valence_panel, weighted, precision=precise)
    screened_term = jnp.einsum("mkv,mc->vkc", direct_rows, conduction_panel, precision=precise)
    band_rows = sum_by_axis(2.0 * bare_term - screened_term, ROW, (0, 2, 1), 0)
    kernel_part = sent_and_summed(band_rows, COL, 2)
    kernel_part = jnp.transpose(kernel_part, (1, 0, 2))
    gaps = conduction_energy[None, None, :] - valence_energy[None, :, None]
    image = gaps * lanczos_now + kernel_part
    inverse_size = 1.0 / (V * C)
    sum_qu, sum_qq, sum_uu, sum_up, sum_pp, sum_qp = (
        one_axis_at_a_time(jnp.sum(lanczos_now * image, axis=(1, 2)), ROW_COL),
        one_axis_at_a_time(jnp.sum(lanczos_now * lanczos_now, axis=(1, 2)), ROW_COL),
        one_axis_at_a_time(jnp.sum(image * image, axis=(1, 2)), ROW_COL),
        one_axis_at_a_time(jnp.sum(image * lanczos_prev, axis=(1, 2)), ROW_COL),
        one_axis_at_a_time(jnp.sum(lanczos_prev * lanczos_prev, axis=(1, 2)), ROW_COL),
        one_axis_at_a_time(jnp.sum(lanczos_now * lanczos_prev, axis=(1, 2)), ROW_COL),
    )
    coef_alpha = sum_qu * inverse_size / (sum_qq * inverse_size + epsilon)
    mean_ww = (
        sum_uu
        - 2.0 * coef_alpha * sum_qu
        - 2.0 * beta_prev * sum_up
        + coef_alpha * coef_alpha * sum_qq
        + beta_prev * beta_prev * sum_pp
        + 2.0 * coef_alpha * beta_prev * sum_qp
    ) * inverse_size
    resid = (
        image - coef_alpha[:, None, None] * lanczos_now - beta_prev[:, None, None] * lanczos_prev
    )
    beta_next = jnp.sqrt(mean_ww + epsilon)
    return (resid / beta_next[:, None, None], jnp.stack([coef_alpha, beta_next], axis=1))


def solution(mesh):
    torus = Mesh(mesh.devices.reshape(4, 2, 4, 4, 2), ("row_0", "row_1", "row_2", "col_0", "col_1"))
    return jax.shard_map(
        per_device,
        mesh=torus,
        in_specs=(
            P(None, ROW, COL),
            P(None, ROW, COL),
            P(),
            P(ROW),
            P(COL),
            P(ROW_COL, None),
            P(ROW_COL, None),
            P(ROW, COL),
            P(ROW, COL),
        ),
        out_specs=(P(None, ROW, COL), P()),
        check_vma=False,
    )
```

profile of v0, /device:TPU:1, one launch (start us, length us, event | category | flops | bytes accessed | tf_op | source)
XLA Modules:
  0.0 726.4 jit_solution(2510422371659446498)
XLA Ops:
  7.2 0.0 all-gather.3.cloned.1.call-start
  7.2 0.7 broadcast_in_dim.4
  7.9 12.2 %all_to_all.20 = f32[8,1,8,128]{3,2,1,0:T(8,128)} all-to-all(f32[8,1,8,128]{3,2,1,0:T(8,128)S(1)} %broadcast_in_dim.4), channel_id=1, replica_groups=mesh['row_0'=4,'row_1'=2,'row_2'=4,'col_0'=4,'col_1'=2] {'col_0','col_1'}, dimensions={0} | all-to-all | bytes 65536 | tf_op jit(solution)/shard_map/all_to_all | solution.py:20
  20.2 0.0 all-gather.3.cloned.1.call-update
  20.2 0.0 all-gather.5.cloned.1.call-start
  20.2 80.5 %all-gather.3.cloned.1.call-done = f32[1,256,1024]{2,1,0:T(8,128)} async-done(((f32[1,8,1024]{2,1,0:T(8,128)}), f32[1,256,1024]{2,1,0:T(8,128)}) %all-gather.3.cloned.1.call-update) | async-done | bytes 1048592 | tf_op jit(solution)/shard_map/all_gather | solution.py:98
  100.7 2.1 fusion.7
  102.9 0.1 copy.21
  103.0 1.5 pad_maximum_fusion.1
  104.5 0.0 all-gather.5.cloned.1.call-update
  104.5 2.4 fusion.9
  106.9 1.1 broadcast_in_dim.5
  108.0 5.7 all-to-all-start.1
  113.7 0.0 reduce-scatter.4.cloned.1.call-start
  113.7 17.8 %all-to-all-done.1 = f32[8,64,1,256]{3,2,1,0:T(1,128)S(1)} async-done(((f32[8,64,1,256]{3,2,1,0:T(1,128)}), f32[8,64,1,256]{3,2,1,0:T(1,128)S(1)}, u32[]{:S(2)}, u32[]{:S(2)}) %all-to-all-start.1) | async-done | bytes 524320 | tf_op jit(solution)/shard_map/all_to_all | solution.py:20
  131.5 406.5 %all-gather.5.cloned.1.call-done = f32[16384,257]{1,0:T(8,128)} async-done(((f32[64,257]{1,0:T(8,128)}), f32[16384,257]{1,0:T(8,128)}) %all-gather.5.cloned.1.call-update) | async-done | bytes 16842768 | tf_op jit(solution)/shard_map/all_gather | solution.py:40
  538.0 0.0 slice-start
  538.0 0.0 copy-start.1
  538.1 3.4 slice-done
  541.4 0.3 dynamic-slice_reduce_fusion
  541.8 0.9 copy-done.1
  542.6 3.4 convolution_bitcast_fusion.1
  546.0 6.5 split.8
  552.5 0.0 copy-start.2
  552.5 3.6 fusion.3
  556.1 0.0 copy-done.2
  556.1 0.0 copy-start.3
  556.1 3.5 fusion
  559.6 0.0 copy-start
  559.6 0.1 pad_maximum_fusion
  559.7 27.3 %all_to_all.21 = f32[8,64,1,257]{3,1,2,0:T(8,128)S(1)} all-to-all(f32[8,64,1,257]{3,1,2,0:T(8,128)S(1)} %pad_maximum_fusion), channel_id=1, replica_groups=mesh['row_0'=4,'row_1'=2,'row_2'=4,'col_0'=4,'col_1'=2] {'col_0','col_1'}, dimensions={0} | all-to-all | bytes 1052672 | tf_op jit(solution)/shard_map/all_to_all | solution.py:50
  587.0 0.0 copy-start.4
  587.0 0.0 copy-start.5
  587.0 0.0 copy-start.6
  587.0 0.0 copy-start.7
  587.0 0.1 slice_reduce_fusion
  587.2 0.0 copy-done.3
  587.2 0.0 copy-done
  587.2 1.1 fusion.5
  588.2 1.1 fusion.6
  589.3 1.1 copy.25
  590.4 0.0 reduce-scatter.4.cloned.1.call-update
  590.4 0.0 reduce-scatter.6.cloned.1.call-start
  590.5 19.3 %reduce-scatter.4.cloned.1.call-done = f32[8,8,1,1024]{3,1,0,2:T(8,128)} async-done(((f32[32,8,1,1024]{3,1,0,2:T(8,128)}), f32[8,8,1,1024]{3,1,0,2:T(8,128)}) %reduce-scatter.4.cloned.1.call-update) | async-done | bytes 262160 | tf_op jit(solution)/shard_map/reduce_scatter | solution.py:70
  609.8 0.0 reduce-scatter.6.cloned.1.call-update
  609.8 0.0 reduce-scatter.8.cloned.1.call-start
  609.8 24.6 %reduce-scatter.6.cloned.1.call-done = f32[2,8,1,1024]{3,1,0,2:T(8,128)} async-done(((f32[8,8,1,1024]{3,1,0,2:T(8,128)}), f32[2,8,1,1024]{3,1,0,2:T(8,128)}) %reduce-scatter.6.cloned.1.call-update) | async-done | bytes 65552 | tf_op jit(solution)/shard_map/reduce_scatter | solution.py:70
  634.4 0.0 reduce-scatter.8.cloned.1.call-update
  634.5 24.0 %reduce-scatter.8.cloned.1.call-done = f32[1,8,1,1024]{3,1,0,2:T(8,128)} async-done(((f32[2,8,1,1024]{3,1,0,2:T(8,128)}), f32[1,8,1,1024]{3,1,0,2:T(8,128)}) %reduce-scatter.8.cloned.1.call-update) | async-done | bytes 32784 | tf_op jit(solution)/shard_map/reduce_scatter | solution.py:70
  658.4 3.7 all-to-all-start.3
  662.8 4.3 all-to-all-done.3
  667.2 0.0 copy-done.4
  667.2 0.0 copy-done.5
  667.2 0.0 copy-done.6
  667.2 0.0 copy-done.7
  667.2 0.8 multiply_reduce_fusion.2
  668.0 9.6 %all-reduce.2 = (f32[1]{0:T(128)}, f32[1]{0:T(128)}, f32[1]{0:T(128)}, f32[1]{0:T(128)}, f32[1]{0:T(128)}, /*index=5*/f32[1]{0:T(128)}) all-reduce(f32[1]{0:T(128)} %bitcast.30, f32[1]{0:T(128)} %bitcast.26, f32[1]{0:T(128)} %bitcast.27, f32[1]{0:T(128)} %bitcast.31, ...), channel_id=1, replica_groups=mesh['row_0'=4,'row_1'=2,'row_2'=4,'col_0'=4,'col_1'=2] {'row_0'}, use_global_device_ids=true, to_apply=%region_19.0 | all-reduce | flops 6 | bytes 48 | tf_op jit(solution)/shard_map/psum | solution.py:81
  677.5 8.4 %all-reduce.4 = (f32[1]{0:T(128)}, f32[1]{0:T(128)}, f32[1]{0:T(128)}, f32[1]{0:T(128)}, f32[1]{0:T(128)}, /*index=5*/f32[1]{0:T(128)}) all-reduce(f32[1]{0:T(128)} %get-tuple-element.20, f32[1]{0:T(128)} %get-tuple-element.21, f32[1]{0:T(128)} %get-tuple-element.22, ...), channel_id=1, replica_groups=mesh['row_0'=4,'row_1'=2,'row_2'=4,'col_0'=4,'col_1'=2] {'row_1'}, use_global_device_ids=true, to_apply=%region_20.0 | all-reduce | flops 6 | bytes 48 | tf_op jit(solution)/shard_map/psum | solution.py:81
  685.9 9.1 %all-reduce.1 = (f32[1]{0:T(128)}, f32[1]{0:T(128)}, f32[1]{0:T(128)}, f32[1]{0:T(128)}, f32[1]{0:T(128)}, /*index=5*/f32[1]{0:T(128)}) all-reduce(f32[1]{0:T(128)} %get-tuple-element.32, f32[1]{0:T(128)} %get-tuple-element.33, f32[1]{0:T(128)} %get-tuple-element.34, ...), channel_id=1, replica_groups=mesh['row_0'=4,'row_1'=2,'row_2'=4,'col_0'=4,'col_1'=2] {'row_2'}, use_global_device_ids=true, to_apply=%region_21.0 | all-reduce | flops 6 | bytes 48 | tf_op jit(solution)/shard_map/psum | solution.py:81
  695.1 7.8 %all-reduce = (f32[1]{0:T(128)}, f32[1]{0:T(128)}, f32[1]{0:T(128)}, f32[1]{0:T(128)}, f32[1]{0:T(128)}, /*index=5*/f32[1]{0:T(128)}) all-reduce(f32[1]{0:T(128)} %get-tuple-element.14, f32[1]{0:T(128)} %get-tuple-element.15, f32[1]{0:T(128)} %get-tuple-element.16, ...), channel_id=1, replica_groups=mesh['row_0'=4,'row_1'=2,'row_2'=4,'col_0'=4,'col_1'=2] {'col_0'}, use_global_device_ids=true, to_apply=%region_22.0 | all-reduce | flops 6 | bytes 48 | tf_op jit(solution)/shard_map/psum | solution.py:81
  702.9 10.7 %all-reduce.3 = (f32[1]{0:T(128)}, f32[1]{0:T(128)}, f32[1]{0:T(128)}, f32[1]{0:T(128)}, f32[1]{0:T(128)}, /*index=5*/f32[1]{0:T(128)}) all-reduce(f32[1]{0:T(128)} %get-tuple-element.8, f32[1]{0:T(128)} %get-tuple-element.9, f32[1]{0:T(128)} %get-tuple-element.10, ...), channel_id=1, replica_groups=mesh['row_0'=4,'row_1'=2,'row_2'=4,'col_0'=4,'col_1'=2] {'col_1'}, use_global_device_ids=true, to_apply=%region_23.0 | all-reduce | flops 6 | bytes 48 | tf_op jit(solution)/shard_map/psum | solution.py:81
  718.6 0.6 pad_maximum_fusion.2
  719.2 0.7 subtract_divide_fusion
  (3 shorter events, 0.1 us)
Async XLA Ops:
  7.2 93.6 %all-gather.3.cloned.1.call-start = ((), (), s32[]{:S(2)}) async-start(), calls=%async_computation.7 | async-start | bytes 1081344 | tf_op jit(solution)/shard_map/all_gather | solution.py:98
  20.2 517.9 %all-gather.5.cloned.1.call-start = ((), (), s32[]{:S(2)}) async-start(), calls=%async_computation.8 | async-start | bytes 25264128 | tf_op jit(solution)/shard_map/all_gather | solution.py:40
  108.0 23.5 %all-to-all-start.1 = ((f32[8,64,1,256]{3,2,1,0:T(1,128)}), f32[8,64,1,256]{3,2,1,0:T(1,128)S(1)}, u32[]{:S(2)}, u32[]{:S(2)}) async-start(f32[8,64,1,256]{3,2,1,0:T(1,128)} %broadcast_in_dim.5), calls=%async_computation.1 | async-start | bytes 1048576 | tf_op jit(solution)/shard_map/all_to_all | solution.py:20
  113.7 496.0 %reduce-scatter.4.cloned.1.call-start = ((), (), s32[]{:S(2)}) async-start(), calls=%async_computation.9 | async-start | bytes 1310720 | tf_op jit(solution)/shard_map/reduce_scatter | solution.py:70
  538.0 3.4 slice-start
  538.0 4.6 copy-start.1
  552.5 3.6 copy-start.2
  556.1 31.0 %copy-start.3 = (f32[64,256]{1,0:T(8,128)S(1)}, f32[64,256]{1,0:T(8,128)}, u32[]{:S(2)}) copy-start(f32[64,256]{1,0:T(8,128)} %param.14) | copy-start | bytes 196612
  559.6 27.6 %copy-start = (f32[64,1024]{1,0:T(8,128)S(1)}, f32[64,1024]{1,0:T(8,128)}, u32[]{:S(2)}) copy-start(f32[64,1024]{1,0:T(8,128)} %param.15) | copy-start | bytes 786436
  587.0 80.2 %copy-start.4 = (f32[1,8,128]{2,1,0:T(8,128)S(1)}, f32[1,8,128]{2,1,0:T(8,128)}, u32[]{:S(2)}) copy-start(f32[1,8,128]{2,1,0:T(8,128)} %param.9) | copy-start | bytes 12292
  587.0 80.2 %copy-start.5 = (f32[1,8,128]{2,1,0:T(8,128)S(1)}, f32[1,8,128]{2,1,0:T(8,128)}, u32[]{:S(2)}) copy-start(f32[1,8,128]{2,1,0:T(8,128)} %param.10) | copy-start | bytes 12292
  587.0 80.2 %copy-start.6 = (f32[8]{0:T(128)S(1)}, f32[8]{0:T(128)}, u32[]{:S(2)}) copy-start(f32[8]{0:T(128)} %param.12) | copy-start | bytes 100
  587.0 80.2 %copy-start.7 = (f32[128]{0:T(128)S(1)}, f32[128]{0:T(128)}, u32[]{:S(2)}) copy-start(f32[128]{0:T(128)} %param.13) | copy-start | bytes 1540
  590.4 44.0 %reduce-scatter.6.cloned.1.call-start = ((), (), s32[]{:S(2)}) async-start(), calls=%async_computation.10 | async-start | bytes 327680 | tf_op jit(solution)/shard_map/reduce_scatter | solution.py:70
  609.8 48.6 %reduce-scatter.8.cloned.1.call-start = ((), (), s32[]{:S(2)}) async-start(), calls=%async_computation.11 | async-start | bytes 98304 | tf_op jit(solution)/shard_map/reduce_scatter | solution.py:70
  658.4 8.7 %all-to-all-start.3 = ((f32[8,8,1,128]{3,1,2,0:T(8,128)}), f32[8,8,1,128]{3,1,2,0:T(8,128)S(1)}, u32[]{:S(2)}, u32[]{:S(2)}) async-start(f32[8,8,1,128]{3,1,2,0:T(8,128)} %bitcast.88), calls=%async_computation.6 | async-start | bytes 65536 | tf_op jit(solution)/shard_map/all_to_all | solution.py:50
Sparse Core Ops, SparseCore 0:
  20.3 80.3 all-gather.2
  104.6 433.3 all-gather.4
  590.5 19.1 reduce-scatter.3
  612.1 22.2 reduce-scatter.5
  636.7 21.6 reduce-scatter.7
where the time goes:
time: 727 us; the launch traced here: 726 us
  waiting for transfers between devices  577 us (79%)
  blocking collectives  85.2 us (12%)
  between operations  19.6 us (3%)
  matrix products  17 us (2%)
  local copies, waits for them, and re-layouts  14.3 us (2%)
  starting transfers between devices  9.62 us (1%)
    all_gather x1, waiting for transfers between devices, sent_together(): lax.all_gather(both, axis, axis=dim, tiled=True)  407 us
    all_gather x1, waiting for transfers between devices, per_device(): vectors = lax.all_gather(wider, ROW, axis=1, tiled=True)  80.5 us
    reduce_scatter x3, waiting for transfers between devices, reduced_to_own(): parts = lax.psum_scatter(parts, axes[k], scatter_dimension=0, tiled=True)  67.8 us
    psum x5, blocking collectives, one_axis_at_a_time(): shard = lax.psum(shard, axis)  45.6 us
    all_to_all x1, blocking collectives, sent_and_summed(): lax.all_to_all(parts, axis, split_axis=0, concat_axis=0, tiled=True)  27.3 us
    all_to_all x1, waiting for transfers between devices, copy_for_each(): return lax.all_to_all(copies, axis, split_axis=0, concat_axis=0, tiled=True)  17.8 us
  transfers between devices with their start and end apart: 7, of which 7 were waited for; matrix products, arithmetic and copies ran while one was open for 0% of the time, Pallas kernels for 0%

commit v1 on v0

v1 whole, which is shorter than its diff:
```python
import functools

import jax
import jax.numpy as jnp
from jax import lax
from jax.experimental import pallas as pl
from jax.experimental.pallas import tpu as pltpu
from jax.sharding import PartitionSpec as P

MESH = pl.DeviceIdType.MESH
HIGHEST = lax.Precision.HIGHEST
V, C = 256, 1024
EPS = 1e-06
NN = (((1,), (0,)), ((), ()))
NT = (((1,), (1,)), ((), ()))
TN = (((0,), (0,)), ((), ()))


def halves(a):
    hi = a.astype(jnp.bfloat16)
    return hi, (a - hi.astype(jnp.float32)).astype(jnp.bfloat16)


def dot3(a, b, dims):
    d = functools.partial(lax.dot_general, dimension_numbers=dims, preferred_element_type=jnp.float32)
    return d(a[0], b[0]) + (d(a[0], b[1]) + d(a[1], b[0]))


def exact(a, b, dims):
    return lax.dot_general(a, b, dims, precision=HIGHEST, preferred_element_type=jnp.float32)


def kernel(
    q_ref, prev_ref, beta_ref, ev_ref, ec_ref, pv_hbm, pc_hbm, w_hbm, b_hbm,
    out_ref, coef_ref,
    w_ref, b_ref, pc_ref, xg, pst, pvc, ar, dst_, dc, sx, s0, s1, kb, r0, r1a, r1b, acc1a, acc1b, r2, acc2, r3,
    mine, tz, mid, txy,
    load_sem, x1s, x1r, x2s, x2r, x3s, x3r, x4s, x4r, p1s, p1r, p2s, p2r, p3s, p3r,
    as_, ar_sem, afs, afr, d1s, d1r, d2s, d2r, d3s, d3r, s0s, s0r, s1s, s1r,
    f0s, f0r, f1s, f1r, f2s, f2r, f3s, f3r, tzs, tzr, txs, txr,
):
    row, col = lax.axis_index("row"), lax.axis_index("col")
    x, zhi, y = row // 8, (row // 4) % 2, row % 4
    zlo, core = col // 2, col % 2
    z = zhi * 4 + zlo
    other = 1 - core

    def dev(px, py, pz, pcore):
        return (px * 8 + (pz // 4) * 4 + py, (pz % 4) * 2 + pcore)

    def rc(src, dst, ss, rs, to):
        return pltpu.make_async_remote_copy(
            src_ref=src, dst_ref=dst, send_sem=ss, recv_sem=rs, device_id=to, device_id_type=MESH
        )

    def px(d):
        return (x + d) % 4

    def py(d):
        return (y + d) % 4

    def pz(d):
        return (z + d) % 8

    partner = dev(x, y, z, other)
    me = dev(x, y, z, core)

    loads = [
        pltpu.make_async_copy(pv_hbm, pst.at[x], load_sem.at[0]),
        pltpu.make_async_copy(pc_hbm, pc_ref, load_sem.at[1]),
        pltpu.make_async_copy(w_hbm, w_ref, load_sem.at[2]),
        pltpu.make_async_copy(b_hbm, b_ref, load_sem.at[3]),
    ]
    for c in loads:
        c.start()

    barrier = pltpu.get_barrier_semaphore()

    def greet(to):
        pl.semaphore_signal(barrier, inc=1, device_id=to, device_id_type=MESH)

    greet(partner)
    for d in range(1, 8):
        greet(dev(x, y, pz(d), core))
        greet(dev(x, y, pz(d), other))
    for d in range(1, 16):
        greet(dev(px(d // 4), py(d % 4), z, core))
    xg[core, x, zhi, y, zlo] = q_ref[0]
    pl.semaphore_wait(barrier, 30)

    def x1(d):
        return rc(q_ref.at[0], xg.at[core, x, zhi, y, zlo], x1s.at[d], x1r.at[d], dev(x, y, pz(d), core))

    for d in range(1, 8):
        x1(d).start()
    loads[0].wait()

    def p1(d):
        return rc(pst.at[x], pst.at[x], p1s.at[d], p1r.at[d], dev(px(d), y, z, core))

    for d in range(1, 4):
        p1(d).start()
    for d in range(1, 8):
        x1(d).wait_recv()

    def x2(d):
        to = dev(jnp.where(core == 0, x, px(d)), jnp.where(core == 0, py(d), y), z, core)
        return rc(xg.at[core, x, :, y], xg.at[core, x, :, y], x2s.at[d], x2r.at[d], to)

    for d in range(1, 4):
        x2(d).start()

    def p2(d, h):
        k = px(-d + 4)
        return rc(
            pst.at[k], pvc.at[y, zlo, core], p2s.at[d * 2 + h], p2r.at[zlo * 2 + core], dev(x, y, k + 4 * h, zhi)
        )

    def p2_self(d, h):
        return (zhi == h) & (px(-d + 4) == zlo) & (core == zhi)

    for d in range(4):
        if d:
            p1(d).wait_recv()
        for h in range(2):

            @pl.when(p2_self(d, h))
            def _():
                pvc[y, zlo, core] = pst[zlo]

            @pl.when(jnp.logical_not(p2_self(d, h)))
            def _():
                p2(d, h).start()

    for d in range(1, 4):
        x2(d).wait_recv()

    def x3a(d):
        return rc(xg.at[core, x], xg.at[core, x], x3s.at[d], x3r.at[d], dev(px(d), y, z, core))

    def x3b(d):
        return rc(xg.at[core, :, :, y], xg.at[core, :, :, y], x3s.at[d], x3r.at[d], dev(x, py(d), z, core))

    def x4a(d):
        part = xg.at[core, px(4 - d)]
        return rc(part, part, x4s.at[d], x4r.at[d], partner)

    def x4b(d):
        part = xg.at[core, :, :, py(4 - d)]
        return rc(part, part, x4s.at[d], x4r.at[d], partner)

    @pl.when(core == 0)
    def _():
        for d in (2, 1, 3):
            x3a(d).start()
        x4a(0).start()

    @pl.when(core == 1)
    def _():
        for d in (2, 1, 3):
            x3b(d).start()
        x4b(0).start()

    for i in range(8):
        own = (i == zlo * 2 + core) & (zhi == core)

        @pl.when(jnp.logical_not(own))
        def _():
            rc(pst.at[0], pvc.at[y, i // 2, i % 2], p2s.at[0], p2r.at[i], partner).wait_recv()

    def p3(up, zl):
        to = dev(x, py(1 if up else 3), z, core)
        j = zl + (0 if up else 4)
        return rc(pvc.at[y, zl], pvc.at[y, zl], p3s.at[j], p3r.at[j], to)

    def p4(up, zl):
        yy = py(3 if up else 1)
        to = dev(x, py(1 if up else 3), z, core)
        j = 8 + zl
        return rc(pvc.at[yy, zl], pvc.at[yy, zl], p3s.at[j], p3r.at[j], to)

    for up, zl in ((1, 0), (0, 2), (1, 1), (0, 3), (1, 2), (0, 0), (1, 3), (0, 1)):
        p3(up, zl).start()

    @pl.when(core == 0)
    def _():
        for d in (1, 3, 2):
            x3a(d).wait_recv()
            x4a(d).start()

    @pl.when(core == 1)
    def _():
        for d in (1, 3, 2):
            x3b(d).wait_recv()
            x4b(d).start()

    for d in range(4):

        @pl.when(core == 0)
        def _():
            part = xg.at[1, :, :, py(4 - d)]
            rc(part, part, x4s.at[d], x4r.at[d], partner).wait_recv()

        @pl.when(core == 1)
        def _():
            part = xg.at[0, px(4 - d)]
            rc(part, part, x4s.at[d], x4r.at[d], partner).wait_recv()

    loads[1].wait()
    xfull = jnp.concatenate([xg[c % 2, :, :, :, c // 2].reshape(V, 128) for c in range(8)], axis=1)
    amp = exact(pc_ref[...], xfull, NT)
    ar[zlo, core] = amp

    def a1(d):
        to = (row, ((zlo + d) % 4) * 2 + core)
        return rc(ar.at[zlo, core], ar.at[zlo, core], as_.at[d], ar_sem.at[d], to)

    def a2(d):
        part = ar.at[(zlo + 4 - d) % 4, core]
        return rc(part, part, afs.at[d], afr.at[d], partner)

    for d in range(1, 4):
        a1(d).start()
    a2(0).start()
    dens = exact(jnp.ones((8, V), jnp.float32), pst[x] * amp, NT)
    dens = jnp.concatenate([dens, dens], axis=1)
    lane8 = lax.broadcasted_iota(jnp.int32, (8, 128), 1)
    dst_[x] = jnp.where(lane8 // 64 == core, dens, 0.0)

    def d1(d):
        return rc(dst_.at[x], dst_.at[x], d1s.at[d], d1r.at[d], dev(px(d), y, z, core))

    for d in range(1, 4):
        d1(d).start()

    def d2(d, h):
        k = px(-d + 4)
        return rc(
            dst_.at[k], dc.at[y, zlo, core], d2s.at[d * 2 + h], d2r.at[zlo * 2 + core], dev(x, y, k + 4 * h, zhi)
        )

    for d in range(4):
        if d:
            d1(d).wait_recv()
        for h in range(2):

            @pl.when(p2_self(d, h))
            def _():
                dc[y, zlo, core] = dst_[zlo]

            @pl.when(jnp.logical_not(p2_self(d, h)))
            def _():
                d2(d, h).start()

    for up, zl in ((1, 0), (0, 2), (1, 1), (0, 3)):
        j = zl + (0 if up else 4)
        yy = py(3 if up else 1)
        rc(pvc.at[yy, zl], pvc.at[yy, zl], p3s.at[j], p3r.at[j], partner).wait_recv()
        p4(up, zl).start()

    for d in range(1, 4):
        part = ar.at[(zlo + 4 - d) % 4, core]
        rc(part, part, as_.at[d], ar_sem.at[d], partner).wait_recv()
        a2(d).start()
    for i in range(8):
        own = (i == zlo * 2 + core) & (zhi == core)

        @pl.when(jnp.logical_not(own))
        def _():
            rc(dst_.at[0], dc.at[y, i // 2, i % 2], d2s.at[0], d2r.at[i], partner).wait_recv()

    def d3(d):
        return rc(dc.at[y], dc.at[y], d3s.at[d], d3r.at[d], dev(x, py(d), z, core))

    for d in range(1, 4):
        d3(d).start()
    for d in range(4):
        part = ar.at[(zlo + 4 - d) % 4, other]
        rc(part, part, afs.at[d], afr.at[d], partner).wait_recv()

    loads[2].wait()
    amps = halves(ar[...].reshape(512, V))
    total = None
    for g in range(4):
        yy = py((0, 3, 1, 2)[g])
        if g == 1:
            for zl in (2, 3):
                rc(pvc.at[yy, zl], pvc.at[yy, zl], p3s.at[0], p3r.at[zl], partner).wait_recv()
        if g == 2:
            for zl in (0, 1):
                rc(pvc.at[yy, zl], pvc.at[yy, zl], p3s.at[0], p3r.at[4 + zl], partner).wait_recv()
        if g == 3:
            for zl in range(4):
                rc(pvc.at[yy, zl], pvc.at[yy, zl], p3s.at[0], p3r.at[8 + zl], partner).wait_recv()
        panel = halves(pvc[yy].reshape(512, V))
        at = pl.ds(pl.multiple_of(yy * 512, 512), 512)
        terms = dot3(amps, panel, NT) * w_ref[:, at]
        part = dot3(halves(terms), panel, NN)
        total = part if total is None else total + part

    sx[:, :, 0:64, :] = total.reshape(4, 2, 64, V)

    for d in range(1, 4):
        part = dc.at[py(4 - d)]
        rc(part, part, d3s.at[d], d3r.at[d], partner).wait_recv()
    loads[3].wait()
    dens_row = dc[:, :, 0, 0:1, :] + dc[:, :, 1, 0:1, :]
    pot = None
    for t in range(16):
        piece = b_ref[:, t * 128 : (t + 1) * 128] * dens_row[t // 4, t % 4]
        pot = piece if pot is None else pot + piece
    pot = jnp.sum(pot, axis=1, keepdims=True)
    sub = lax.broadcasted_iota(jnp.int32, (64, 128), 0)
    lane = lax.broadcasted_iota(jnp.int32, (64, 128), 1)
    diag = sub == lane
    for j in range(8):
        line = jnp.sum(jnp.where(diag, pot[j * 64 : (j + 1) * 64], 0.0), axis=0, keepdims=True)
        line = jnp.concatenate([jnp.broadcast_to(line, (8, 128)), jnp.zeros((8, 128), jnp.float32)], axis=1)
        sx[j // 2, j % 2, 64:72, :] = line

    def sa(zl):
        return rc(sx.at[zl, other], s0.at[zl], s0s.at[zl], s0r.at[zl], partner)

    def sb(d):
        zl = (zlo + d) % 4
        return rc(sx.at[zl, core], s1.at[d], s1s.at[d], s1r.at[d], (row, zl * 2 + core))

    order = [(zlo + d) % 4 for d in (2, 1, 3, 0)]
    for zl in order:
        sa(zl).start()
    for d, zl in zip((2, 1, 3, 0), order):
        sa(zl).wait_recv()
        sx[zl, core] = sx[zl, core] + s0[zl]
        if d:
            sb(d).start()
    for d in range(1, 4):
        sb(d).wait_recv()
    mine_s = sx[zlo, core] + s1[1] + s1[2] + s1[3]

    pot_row = mine_s[64:65, 0:128]
    pot_col = jnp.sum(jnp.where(diag, pot_row, 0.0), axis=1, keepdims=True)
    both = 2.0 * pot_col * pst[x] - mine_s[0:64]
    kpart = exact(both, pc_ref[...], TN)
    for c in range(8):
        kb[c % 2, :, :, :, c // 2] = kpart[:, c * 128 : (c + 1) * 128].reshape(4, 2, 4, 8, 128)

    def f0(i):
        return rc(kb.at[other, i], r0.at[i], f0s.at[i], f0r.at[i], partner)

    for i in range(4):
        f0(i).start()
    for i in range(4):
        f0(i).wait_recv()
        kb[core, i] = kb[core, i] + r0[i]

    def f1a(d):
        return rc(kb.at[core, px(d)], r1a.at[d - 1], f1s.at[d], f1r.at[d], dev(px(d), y, z, core))

    def f1b(d):
        return rc(kb.at[core, :, :, py(d)], r1b.at[d - 1], f1s.at[d], f1r.at[d], dev(x, py(d), z, core))

    def f2a(d):
        return rc(acc1a.at[:, py(d)], r2.at[d - 1], f2s.at[d], f2r.at[d], dev(x, py(d), z, core))

    def f2b(d):
        return rc(acc1b.at[px(d)], r2.at[d - 1], f2s.at[d], f2r.at[d], dev(px(d), y, z, core))

    @pl.when(core == 0)
    def _():
        for d in (2, 1, 3):
            f1a(d).start()
        for d in range(1, 4):
            f1a(d).wait_recv()
        acc1a[...] = kb[0, x] + r1a[0] + r1a[1] + r1a[2]
        for d in (2, 1, 3):
            f2a(d).start()
        for d in range(1, 4):
            f2a(d).wait_recv()
        acc2[...] = acc1a[:, y] + r2[0] + r2[1] + r2[2]

    @pl.when(core == 1)
    def _():
        for d in (2, 1, 3):
            f1b(d).start()
        for d in range(1, 4):
            f1b(d).wait_recv()
        acc1b[...] = kb[1, :, :, y] + r1b[0] + r1b[1] + r1b[2]
        for d in (2, 1, 3):
            f2b(d).start()
        for d in range(1, 4):
            f2b(d).wait_recv()
        acc2[...] = acc1b[x] + r2[0] + r2[1] + r2[2]

    def f3(d):
        zz = pz(d)
        return rc(acc2.at[zz // 4, zz % 4], r3.at[d], f3s.at[d], f3r.at[d], dev(x, y, zz, core))

    for d in range(1, 8):
        f3(d).start()
    for d in range(1, 8):
        f3(d).wait_recv()
    tile = acc2[zhi, zlo]
    for d in range(1, 8):
        tile = tile + r3[d]

    q, prev = q_ref[0], prev_ref[0]
    sub8 = lax.broadcasted_iota(jnp.int32, (8, 128), 0)
    ev = jnp.zeros((8, 128), jnp.float32)
    for i in range(8):
        ev = jnp.where(sub8 == i, ev_ref[i], ev)
    ec = ec_ref[...].reshape(1, 128)
    image = (ec - ev) * q + tile
    sums = jnp.zeros((8, 128), jnp.float32)
    for i, term in enumerate((q * image, q * q, image * image, image * prev, prev * prev, q * prev)):
        sums = jnp.where(sub8 == i, jnp.sum(term, axis=0, keepdims=True), sums)
    mine[...] = sums

    def t1(j):
        d, c = j % 8, j // 8
        return rc(mine, tz.at[j], tzs.at[j], tzr.at[j], dev(x, y, pz(d), core if c == 0 else other))

    for j in range(1, 16):
        t1(j).start()
    for j in range(1, 16):
        t1(j).wait_recv()
    part = sums
    for j in range(1, 16):
        part = part + tz[j]
    mid[...] = part

    def t2(j):
        return rc(mid, txy.at[j], txs.at[j], txr.at[j], dev(px(j // 4), py(j % 4), z, core))

    for j in range(1, 16):
        t2(j).start()
    for j in range(1, 16):
        t2(j).wait_recv()
    for j in range(1, 16):
        part = part + txy[j]
    part = jnp.sum(part, axis=1, keepdims=True)
    qu, qq, uu, up_, pp, qp = (part[i : i + 1] for i in range(6))
    inv = 1.0 / (V * C)
    bp = beta_ref[0]
    alpha = qu * inv / (qq * inv + EPS)
    ww = (
        uu - 2.0 * alpha * qu - 2.0 * bp * up_ + alpha * alpha * qq + bp * bp * pp + 2.0 * alpha * bp * qp
    ) * inv
    beta = jnp.sqrt(ww + EPS)
    out_ref[0] = (image - alpha * q - bp * prev) / beta
    two = lax.broadcasted_iota(jnp.int32, (1, 2), 1)
    coef_ref[...] = jnp.where(two == 0, alpha, beta)

    for d in range(1, 8):
        x1(d).wait_send()
        f3(d).wait_send()
    for d in range(1, 4):
        x2(d).wait_send()
        p1(d).wait_send()
        a1(d).wait_send()
        d1(d).wait_send()
        d3(d).wait_send()
        sb(d).wait_send()
    for d in range(4):
        a2(d).wait_send()
        f0(d).wait_send()
        sa(d).wait_send()
        for h in range(2):

            @pl.when(jnp.logical_not(p2_self(d, h)))
            def _():
                p2(d, h).wait_send()
                d2(d, h).wait_send()

    for zl in range(4):
        p3(1, zl).wait_send()
        p3(0, zl).wait_send()
        p4(1 if zl < 2 else 0, zl).wait_send()

    @pl.when(core == 0)
    def _():
        for d in range(4):
            x4a(d).wait_send()
            if d:
                x3a(d).wait_send()
                f1a(d).wait_send()
                f2a(d).wait_send()

    @pl.when(core == 1)
    def _():
        for d in range(4):
            x4b(d).wait_send()
            if d:
                x3b(d).wait_send()
                f1b(d).wait_send()
                f2b(d).wait_send()

    for j in range(1, 16):
        t1(j).wait_send()
        t2(j).wait_send()


def per_device(q, prev, beta, ev, ec, pv, pc, w, b):
    f32 = jnp.float32
    vmem = pl.BlockSpec(memory_space=pltpu.VMEM)
    smem = pl.BlockSpec(memory_space=pltpu.SMEM)
    hbm = pl.BlockSpec(memory_space=pl.ANY)

    def buf(*shape):
        return pltpu.VMEM(shape, f32)

    def sem(n):
        return pltpu.SemaphoreType.DMA((n,))

    tile = (8, 128)
    scratch = [
        buf(512, 2048), buf(512, 2048), buf(64, C),
        buf(2, 4, 2, 4, 4, *tile),
        buf(4, 64, V), buf(4, 4, 2, 64, V),
        buf(4, 2, 64, V),
        buf(4, *tile), buf(4, 4, 2, *tile),
        buf(4, 2, 72, V), buf(4, 72, V), buf(4, 72, V),
        buf(2, 4, 2, 4, 4, *tile), buf(4, 2, 4, 4, *tile),
        buf(3, 2, 4, 4, *tile), buf(3, 4, 2, 4, *tile),
        buf(2, 4, 4, *tile), buf(4, 2, 4, *tile),
        buf(3, 2, 4, *tile), buf(2, 4, *tile), buf(8, *tile),
        buf(*tile), buf(16, *tile), buf(*tile), buf(16, *tile),
        sem(4),
        sem(8), sem(8), sem(4), sem(4), sem(4), sem(4), sem(4), sem(4),
        sem(4), sem(4), sem(8), sem(8), sem(12), sem(12),
        sem(4), sem(4), sem(4), sem(4),
        sem(4), sem(4), sem(8), sem(8), sem(4), sem(4),
        sem(4), sem(4), sem(4), sem(4),
        sem(4), sem(4), sem(4), sem(4), sem(4), sem(4), sem(8), sem(8),
        sem(16), sem(16), sem(16), sem(16),
    ]
    return pl.pallas_call(
        kernel,
        out_shape=(jax.ShapeDtypeStruct((1, 8, 128), f32), jax.ShapeDtypeStruct((1, 2), f32)),
        in_specs=[vmem, vmem, smem, smem, vmem, hbm, hbm, hbm, hbm],
        out_specs=(vmem, vmem),
        scratch_shapes=scratch,
        compiler_params=pltpu.CompilerParams(
            collective_id=0, has_side_effects=True, vmem_limit_bytes=60 * 1024 * 1024
        ),
        name="lanczos_step",
    )(q, prev, beta, ev, ec, pv, pc, w, b)


def solution(mesh):
    return jax.shard_map(
        per_device,
        mesh=mesh,
        in_specs=(
            P(None, "row", "col"),
            P(None, "row", "col"),
            P(),
            P("row"),
            P("col"),
            P(("row", "col"), None),
            P(("row", "col"), None),
            P("row", "col"),
            P("row", "col"),
        ),
        out_specs=(P(None, "row", "col"), P()),
        check_vma=False,
    )
```

time: 727 us -> 91.4 us (0.13)
  waiting for transfers between devices: 577 us -> 0 us
  Pallas kernels: 0 us -> 87.5 us
  blocking collectives: 85.2 us -> 0 us
  between operations: 19.6 us -> 1.29 us
  matrix products: 17 us -> 0 us
  local copies, waits for them, and re-layouts: 14.3 us -> 2.4 us
  starting transfers between devices: 9.62 us -> 0 us
    all_gather x2 -> x0, waiting for transfers between devices: 487 us -> none  [the longest x1 407 us: sent_together(): lax.all_gather(both, axis, axis=dim, tiled=True)]
    pallas_call x0 -> x1, Pallas kernels: none -> 87.5 us  [per_device(): pl.pallas_call(kernel, out_shape=(jax.ShapeDtypeStruct((1, 8, 128), f32),...]
    reduce_scatter x3 -> x0, waiting for transfers between devices: 67.8 us -> none  [reduced_to_own(): parts = lax.psum_scatter(parts, axes[k], scatter_dimension=0, tiled=True)]
    psum x5 -> x0, blocking collectives: 45.6 us -> none  [one_axis_at_a_time(): shard = lax.psum(shard, axis)]
    all_to_all x2 -> x0, blocking collectives: 39.6 us -> none  [the longest x1 27.3 us: sent_and_summed(): lax.all_to_all(parts, axis, split_axis=0, concat_axis=0, tiled=True)]
    all_to_all x2 -> x0, waiting for transfers between devices: 22.1 us -> none  [the longest x1 17.8 us: copy_for_each(): return lax.all_to_all(copies, axis, split_axis=0, concat_axis=0, tiled=True)]
    dot_general x7 -> x0, matrix products: 17 us -> none  [the longest x1 3.55 us: per_device(): jnp.einsum('mkv,nv->mkn', gather_directly(pair_local, COL, 0), panel, pre...]
    split x3 -> x0, local copies, waits for them, and re-layouts: 9.87 us -> none  [sent_together(): jnp.split(lax.all_gather(both, axis, axis=dim, tiled=True), ends, axis=al...]
  transfers between devices with their start and end apart: 7 -> 0, of which waited for: 7 -> 0; matrix products, arithmetic and copies ran while one was open for 0% -> 0% of each run, Pallas kernels for 0% -> 0%
where the time goes in v1:
time: 91.4 us; the launch traced here: 91.2 us
  Pallas kernels  87.5 us (96%)
  local copies, waits for them, and re-layouts  2.4 us (3%)
  between operations  1.29 us (1%)
    pallas_call x1, Pallas kernels, per_device(): pl.pallas_call(kernel, out_shape=(jax.ShapeDtypeStruct((1, 8, 128), f32),...  87.5 us
    unnamed x2, local copies, waits for them, and re-layouts  2.4 us

profile of v1, /device:TPU:1, one launch (start us, length us, event | category | flops | bytes accessed | tf_op | source)
XLA Modules:
  0.0 91.2 jit_solution(1407904767303416805)
XLA Ops:
  1.3 87.5 %lanczos_step.1 = (f32[1,8,128]{2,1,0:T(8,128)}, f32[1,2]{1,0:T(1,128)}) custom-call(f32[1,8,128]{2,1,0:T(8,128)} %q_ref.1, f32[1,8,128]{2,1,0:T(8,128)} %prev_ref.1, f32[1]{0:T(128)S(6)} %copy.13.beta_ref, f32[8]{0:T(128)} %ev_ref.1, f32[128]{0:T(128)} %ec_ref.1, f32[64,256]{1,0:T(8,128)} %pv_hbm.1, f32[64,1024]{1,0:T(8,128)} %pc_hbm.1, f32[512,2048]{1,0:T(8,128)} %w_hbm.1, ...), custom_call_target="tpu_custom_call" | custom-call | tf_op jit(solution)/shard_map/lanczos_step/pallas_call | solution.py:536
  88.8 1.3 %copy.14 = f32[1,8,128]{2,1,0:T(8,128)} copy(f32[1,8,128]{2,1,0:T(8,128)} %get-tuple-element.4) | data formatting | bytes 8192
  90.1 1.1 %copy.15 = f32[1,2]{1,0:T(1,128)} copy(f32[1,2]{1,0:T(1,128)} %get-tuple-element.5) | data formatting | bytes 16

commit v2 on v0

v2 whole, which is shorter than its diff:
```python
import functools

import jax
import jax.numpy as jnp
from jax import lax
from jax.experimental import pallas as pl
from jax.experimental.pallas import tpu as pltpu
from jax.sharding import PartitionSpec as P

MESH = pl.DeviceIdType.MESH
HIGHEST = lax.Precision.HIGHEST
V, C = 256, 1024
EPS = 1e-06
NN = (((1,), (0,)), ((), ()))
NT = (((1,), (1,)), ((), ()))
TN = (((0,), (0,)), ((), ()))


def halves(a):
    hi = a.astype(jnp.bfloat16)
    return hi, (a - hi.astype(jnp.float32)).astype(jnp.bfloat16)


def left3(a, axis):
    hi, lo = halves(a)
    return jnp.concatenate([hi, lo, hi], axis=axis)


def right3(a, axis):
    hi, lo = halves(a)
    return jnp.concatenate([hi, hi, lo], axis=axis)


def dot(a, b, dims):
    return lax.dot_general(a, b, dims, preferred_element_type=jnp.float32)


def exact(a, b, dims):
    return lax.dot_general(a, b, dims, precision=HIGHEST, preferred_element_type=jnp.float32)


def kernel(
    beta_hbm, ev_hbm, q_hbm, prev_hbm, ec_hbm, pv_hbm, pc_hbm, w_hbm, b_hbm,
    out_ref, coef_ref,
    beta_ref, ev_ref, ec_ref, q_ref, prev_ref, own_pv, pc_other, w_ref, b_ref, pcr, pch, pcl, pvr, xg, pvc, ph, pl_,
    ap, ao, asum, amps, dmine, dc, potx, pot0, ee, eo, dd, kb, r1a, r1b, acc1, r3,
    tz, txy, az, axy, mid, amid, dummy,
    load_sem, send_sem,
    x1r, x2r, x3r, p2r, p3r, p4r, p5r, cr, vr, v2r, ar_, dr, q0r, er, f1r, f3r, tr,
):
    row, col = lax.axis_index("row"), lax.axis_index("col")
    x, zhi, y = row // 8, (row // 4) % 2, row % 4
    zlo, core = col // 2, col % 2
    z = zhi * 4 + zlo
    other = 1 - core
    a, b = jnp.where(core == 0, y, x), jnp.where(core == 0, x, y)

    def dev(px, py, pz, pcore):
        return (px * 8 + (pz // 4) * 4 + py, (pz % 4) * 2 + pcore)

    def rc(src, dst, group, rs, to):
        return pltpu.make_async_remote_copy(
            src_ref=src, dst_ref=dst, send_sem=send_sem.at[group], recv_sem=rs, device_id=to, device_id_type=MESH
        )

    def px(d):
        return (x + d) % 4

    def py(d):
        return (y + d) % 4

    def pz(d):
        return (z + d) % 8

    def ab(da, db, dz=0):
        ja, jb = (a + da) % 4, (b + db) % 4
        return dev(jnp.where(core == 0, jb, ja), jnp.where(core == 0, ja, jb), pz(dz), core)

    partner = dev(x, y, z, other)

    def arrived(rs, kib):
        part = dummy.at[pl.ds(0, kib * 2)]
        rc(part, part, 0, rs, partner).wait_recv()

    def left(group, kib):
        part = dummy.at[pl.ds(0, kib * 2)]
        rc(part, part, group, x1r, partner).wait_send()

    def rows_arrived(rs, ref, n):
        part = ref.at[pl.ds(0, n)]
        rc(part, part, 0, rs, partner).wait_recv()

    def rows_left(group, ref, n):
        part = ref.at[pl.ds(0, n)]
        rc(part, part, group, x1r, partner).wait_send()

    lanes = [slice(c * 128, (c + 1) * 128) for c in range(4)]
    pairs = [(q_hbm, q_ref), (pv_hbm, own_pv)]
    for c in range(4):
        mine, its = (pl.ds(pl.multiple_of((c * 2 + k) * 128, 128), 128) for k in (core, other))
        pairs.append((pc_hbm.at[:, mine], pcr.at[zlo, core, :, lanes[c]]))
        pairs.append((pc_hbm.at[:, its], pc_other.at[:, lanes[c]]))
    pairs += [(prev_hbm, prev_ref), (ec_hbm, ec_ref), (ev_hbm, ev_ref), (beta_hbm, beta_ref)]
    pairs += [(w_hbm, w_ref), (b_hbm, b_ref)]
    loads = [pltpu.make_async_copy(s, d, load_sem.at[i]) for i, (s, d) in enumerate(pairs)]
    for c in loads:
        c.start()

    barrier = pltpu.get_barrier_semaphore()

    def greet(to):
        pl.semaphore_signal(barrier, inc=1, device_id=to, device_id_type=MESH)

    in_own_block = (x == zlo) & (core == zhi)
    for i in range(8):
        to = dev(zlo, y, core * 4 + (zlo + i // 2) % 4, (core + i % 2) % 2)
        if i == 0:

            @pl.when(jnp.logical_not(in_own_block))
            def _():
                greet(to)

        else:
            greet(to)
    for d in range(1, 4):
        greet(dev(px(d), y, z, core))
        greet(dev(x, py(d), z, core))
    for d in (4, 3, 5, 2, 6, 1, 7):
        greet(dev(x, y, pz(d), core))
        greet(dev(x, y, pz(d), other))
    greet(partner)
    loads[0].wait()
    xg[x, zhi, y, zlo] = q_ref[0]
    for i in range(1, 10):
        loads[i].wait()
    pvr[zlo, core] = own_pv[...]

    @pl.when(in_own_block)
    def _():
        pvc[y, zlo * 2 + core, x] = own_pv[pl.ds(pl.multiple_of(x * 16, 16), 16)]
        pl.semaphore_wait(barrier, 21 + 7)

    @pl.when(jnp.logical_not(in_own_block))
    def _():
        pl.semaphore_wait(barrier, 21 + 8)

    for d in (4, 3, 5, 2, 6, 1, 7):
        rc(q_ref.at[0], xg.at[x, zhi, y, zlo], 0, x1r, dev(x, y, pz(d), core)).start()

    for i in range(8):
        quarter, to = px(i // 2), dev(px(i // 2), y, x + 4 * ((zhi + i % 2) % 2), zhi)
        part = own_pv.at[pl.ds(pl.multiple_of(quarter * 16, 16), 16)]
        copy = rc(part, pvc.at[y, zlo * 2 + core, quarter], 2, p2r, to)
        if i == 0:
            pl.when(jnp.logical_not(in_own_block))(copy.start)
        else:
            copy.start()

    def block_wait(wait, sem, per, n, *rest):
        @pl.when(in_own_block)
        def _():
            wait(sem, *rest, per * (n - 1))

        @pl.when(jnp.logical_not(in_own_block))
        def _():
            wait(sem, *rest, per * n)

    def inside(s):
        return (zlo + s >= 0) & (zlo + s < 4)

    own_rows = pcr.at[zlo, core]
    rc(pc_other, own_rows, 1, cr.at[0], partner).start()
    def rows_came(s):
        arrived(cr.at[s] if s > 0 else cr.at[3 - s], 256)

    arrived(x1r, 28)

    part = xg.at[x, :, y]
    for d in (2, 1, 3):
        rc(part, part, 0, x2r, ab(d, 0)).start()

    block_wait(arrived, p2r, 16, 8)
    def unit(da, db):
        ja, jb = (a + da) % 4, (b + db) % 4
        return pvc.at[jnp.where(core == 0, ja, jb), :, jnp.where(core == 0, jb, ja)]

    def p3(d):
        return rc(unit(0, 0), unit(0, 0), 5, p3r.at[d], ab(d, 0))

    def p4(up, rel):
        part = unit(rel, 0)
        return rc(part, part, 6, p4r.at[up * 4 + rel], ab(0, 1 if up else 3))

    def p4_came(up, rel):
        part = unit(rel, 3 if up else 1)
        rc(part, part, 6, p4r.at[up * 4 + rel], partner).wait_recv()

    def p5(up, rel):
        part = unit(rel, 3 if up else 1)
        return rc(part, part, 7, p5r, ab(0, 1 if up else 3))

    for d in (2, 1, 3):
        p3(d).start()
    for s in (2, -2, 1, -1):

        @pl.when(inside(s))
        def _():
            rc(own_rows, own_rows, 3, cr.at[abs(s)] if s > 0 else cr.at[3 + abs(s)], (row, (zlo + s) * 2 + core)).start()
            rc(pc_other, own_rows, 3, cr.at[abs(s)] if s > 0 else cr.at[3 + abs(s)], (row, (zlo + s) * 2 + other)).start()

    for s in (2, -2, 1, -1):

        @pl.when(inside(s))
        def _():
            rc(pvr.at[zlo, core], pvr.at[zlo, core], 4, vr.at[s + 3], (row, (zlo + s) * 2 + core)).start()

    arrived(x2r, 96)

    def chunk(c, d):
        return xg.at[px(d)] if c == 0 else xg.at[:, :, py(d)]

    for c in range(2):

        @pl.when(core == c)
        def _():
            for d in (2, 1, 3):
                rc(chunk(c, 0), chunk(c, 0), 8, x3r, ab(0, d)).start()

    p4(1, 0).start()
    p4(0, 0).start()

    for d in (1, 3, 2):
        part = unit(4 - d, 0)
        rc(part, part, 5, p3r.at[d], partner).wait_recv()
        p4(1, 4 - d).start()
        p4(0, 4 - d).start()

    arrived(x3r, 384)
    arrived(cr.at[0], 128)

    xs = left3(jnp.concatenate([xg[:, :, :, c].reshape(V, 128) for c in range(4)], axis=1), 1)

    def a1(zl):
        return rc(ap.at[zl], ao.at[zl], 10, ar_.at[zl], partner)

    def amp_of(zl):
        at = pl.ds(pl.multiple_of(zl * 128, 128), 128)
        hi, lo = halves(pcr[zl].reshape(128, 512))
        pch[at] = hi
        pcl[at] = lo
        ap[zl] = dot(jnp.concatenate([hi, hi, lo], axis=1), xs, NT).reshape(2, 64, V)
        a1(zl).start()

    amp_of(zlo)

    def relays(s):
        return inside(-s) & inside(s // 2)

    for s in (2, -2):

        @pl.when(relays(s))
        def _():
            rows_came(s)
            part = pcr.at[zlo - s]
            rc(part, part, 9, cr.at[3] if s > 0 else cr.at[6], (row, (zlo + s // 2) * 2 + core)).start()

    for up, rel in ((1, 0), (0, 3)):
        p4_came(up, rel)
        p5(up, rel).start()

    a1(zlo).wait_recv()
    own_amp = ap[zlo, core] + ao[zlo, core]
    dens = exact(jnp.ones((8, V), jnp.float32), own_pv[...] * own_amp, NT)[0:1]
    dens = jnp.concatenate([dens, dens], axis=1)
    lane1 = lax.broadcasted_iota(jnp.int32, (1, 128), 1)
    dmine[...] = jnp.where(lane1 // 64 == core, dens, 0.0)
    slot = y * 8 + zlo * 2 + core
    for i in range(32):
        to = dev(px(2 + i // 8), py(2 + (i // 2) % 4), x + 4 * ((zhi + i % 2) % 2), zhi)
        copy = rc(dmine, dc.at[slot], 11, dr, to)
        if i == 20:

            @pl.when(in_own_block)
            def _():
                dc[slot] = dmine[...]

            pl.when(jnp.logical_not(in_own_block))(copy.start)
        else:
            copy.start()

    for up, rel in ((1, 1), (0, 2)):
        p4_came(up, rel)
        p5(up, rel).start()

    for s in (2, -2):

        @pl.when(inside(-s) & jnp.logical_not(relays(s)))
        def _():
            rows_came(s)

        @pl.when(inside(-s))
        def _():
            amp_of(zlo - s)

    for s in (1, -1):

        @pl.when(inside(-s))
        def _():
            rows_came(s)
            amp_of(zlo - s)

    def v_came(s):
        part = pvr.at[zlo - s, core]
        rc(part, part, 4, vr.at[s + 3], partner).wait_recv()

    def v2(s):
        part = pvr.at[zlo - s, core]
        return rc(part, part, 14, v2r, partner)

    v2(0).start()
    for s in (2, -2, 1, -1):

        @pl.when(inside(-s))
        def _():
            v_came(s)
            v2(s).start()

        if abs(s) == 2:

            @pl.when(relays(s))
            def _():
                part = pvr.at[zlo - s, core]
                rc(part, part, 12, vr.at[s // 2 * 3 + 3], (row, (zlo + s // 2) * 2 + core)).start()

    for s in (3, -3):

        @pl.when(inside(-s))
        def _():
            rows_came(s)
            amp_of(zlo - s)

    for up, rel in ((1, 3), (1, 2), (0, 0), (0, 1)):
        p4_came(up, rel)
    arrived(p5r, 512)
    loads[14].wait()
    hi, lo = halves(pvc[...].reshape(2048, V))
    ph[...] = hi
    pl_[...] = lo
    for d in range(1, 4):
        a1((zlo + d) % 4).wait_recv()
    asum[...] = ap[...] + ao[...]
    amps[...] = left3(asum[...].reshape(512, V), 1)

    def block(g, rows):
        at = slice(g * 512, (g + 1) * 512)
        hi, lo = ph[at], pl_[at]
        terms = dot(amps[rows], jnp.concatenate([hi, hi, lo], axis=1), NT) * w_ref[rows, at]
        return dot(left3(terms, 1), jnp.concatenate([hi, hi, lo], axis=0), NN)

    def e1(i):
        part = pl.ds(2 * i, 2)
        return rc(ee.at[part], eo.at[part], 13, er.at[i], partner)

    def half(i):
        rows = slice(i * 256, (i + 1) * 256)
        part = block(0, rows) + block(1, rows) + block(2, rows) + block(3, rows)
        ee[2 * i : 2 * i + 2] = part.reshape(2, 2, 64, V)
        e1(i).start()

    half(0)

    loads[15].wait()
    block_wait(rows_arrived, dr, 1, 32, dc)
    pot = None
    for t in range(16):
        piece = b_ref[:, t * 128 : (t + 1) * 128] * (dc[2 * t] + dc[2 * t + 1])
        pot = piece if pot is None else pot + piece
    potx[...] = jnp.broadcast_to(jnp.sum(pot, axis=1, keepdims=True), (512, 128)).reshape(4, 2, 64, 128)

    def q0():
        return rc(potx, pot0, 15, q0r, partner)

    q0().start()
    half(1)

    for s in (3, -3):

        @pl.when(inside(-s))
        def _():
            v_came(s)
            v2(s).start()

    q0().wait_recv()
    arrived(v2r, 256)

    def kpart(i):
        e1(i).wait_recv()
        at = slice(2 * i, 2 * i + 2)
        pot2 = 2.0 * (potx[at] + pot0[at])
        both = jnp.concatenate([pot2, pot2], axis=3) * pvr[at] - (ee[at] + eo[at])
        dd[at] = both
        rows = slice(i * 256, (i + 1) * 256)
        hi, lo = pch[rows], pcl[rows]
        return dot(left3(both.reshape(256, V), 0), jnp.concatenate([hi, hi, lo], axis=0), TN)

    kfull = kpart(0)
    kfull = kfull + kpart(1)
    for c in range(4):
        kb[:, :, :, c] = kfull[:, lanes[c]].reshape(4, 2, 4, 8, 128)

    for c in range(2):

        @pl.when(core == c)
        def _():
            for d in (2, 1, 3):
                part = kb.at[px(d)] if c == 0 else kb.at[:, :, py(d)]
                rc(part, (r1a if c == 0 else r1b).at[d - 1], 16, f1r, ab(0, d)).start()

    for i in (10, 11, 12, 13):
        loads[i].wait()
    q, prev = q_ref[0], prev_ref[0]
    sub8 = lax.broadcasted_iota(jnp.int32, (8, 128), 0)
    ev = jnp.zeros((8, 128), jnp.float32)
    for i in range(8):
        ev = jnp.where(sub8 == i, ev_ref[i], ev)
    gaps = ec_ref[...].reshape(1, 128) - ev
    prod = (dd[:, core] * asum[:, core]).reshape(256, V)
    prod = jnp.sum(prod[:, 0:128] + prod[:, 128:256], axis=0, keepdims=True)
    qq = jnp.sum(q * q, axis=0, keepdims=True)
    qu = prod + jnp.sum(gaps * q * q, axis=0, keepdims=True)
    az[0] = jnp.concatenate([qu, qq], axis=1)

    def t1(src, dst, group, rs):
        for d in (4, 3, 5, 2, 6, 1, 7, 0):
            for j in (d, d + 8):
                if j:
                    to = dev(x, y, pz(d), core if j < 8 else other)
                    rc(src, dst.at[j], group, rs, to).start()

    def t2(src, dst, group, rs):
        for j in (10, 9, 11, 6, 14, 2, 8, 5, 7, 13, 15, 1, 3, 4, 12):
            rc(src, dst.at[j], group, rs, dev(px(j // 4), py(j % 4), z, core)).start()

    t1(az.at[0], az, 18, tr.at[0])

    arrived(f1r, 384)
    for c in range(2):

        @pl.when(core == c)
        def _():
            if c == 0:
                for i in range(2):
                    acc1[:, i] = kb[x, i] + r1a[0, i] + r1a[1, i] + r1a[2, i]
            else:
                acc1[...] = kb[:, :, y] + r1b[0] + r1b[1] + r1b[2]

    for da in (2, 1, 3, 0):
        for dz in (4, 3, 5, 2, 6, 1, 7, 0):
            if da or dz:
                zz = pz(dz)
                part = acc1.at[(a + da) % 4, zz // 4, zz % 4]
                rc(part, r3.at[da * 8 + dz], 17, f3r, ab(da, 0, dz)).start()
    rows_arrived(tr.at[0], az, 15)
    amid[...] = jnp.sum(az[...], axis=0)
    axy[0] = amid[...]
    t2(amid, axy, 19, tr.at[1])
    arrived(f3r, 124)
    tile = acc1[a, zhi, zlo] + jnp.sum(r3[1:32], axis=0)
    inv = 1.0 / (V * C)
    bp = beta_ref[0]
    rows_arrived(tr.at[1], axy, 15)
    total = jnp.sum(axy[...], axis=0)
    qu = jnp.sum(total[:, 0:128], axis=1, keepdims=True)
    qq = jnp.sum(total[:, 128:256], axis=1, keepdims=True)
    alpha = qu * inv / (qq * inv + EPS)
    resid = tile + (gaps - alpha) * q - bp * prev
    tz[0] = jnp.sum(resid * resid, axis=0, keepdims=True)
    t1(tz.at[0], tz, 20, tr.at[2])
    rows_arrived(tr.at[2], tz, 15)
    mid[...] = jnp.sum(tz[...], axis=0)
    t2(mid, txy, 21, tr.at[3])
    txy[0] = mid[...]
    rows_arrived(tr.at[3], txy, 15)
    ww = jnp.sum(jnp.sum(txy[...], axis=0), axis=1, keepdims=True)
    beta = jnp.sqrt(ww * inv + EPS)
    out_ref[0] = resid / beta
    two = lax.broadcasted_iota(jnp.int32, (1, 2), 1)
    coef_ref[...] = jnp.where(two == 0, alpha, beta)

    left(0, 124)
    left(1, 128)
    block_wait(left, 2, 16, 8)
    left(5, 384)
    left(6, 1024)
    left(7, 512)
    left(8, 384)

    @pl.when((zlo == 0) | (zlo == 3))
    def _():
        left(3, 512)
        left(4, 128)

    @pl.when((zlo == 1) | (zlo == 2))
    def _():
        left(3, 768)
        left(4, 192)
        left(9, 256)
        left(12, 64)

    left(10, 512)
    block_wait(rows_left, 11, 1, 32, dc)
    left(13, 512)
    left(14, 256)
    left(15, 256)
    left(16, 384)
    left(17, 124)
    rows_left(18, az, 15)
    rows_left(19, axy, 15)
    rows_left(20, tz, 15)
    rows_left(21, txy, 15)


def per_device(q, prev, beta, ev, ec, pv, pc, w, b):
    f32 = jnp.float32
    vmem = pl.BlockSpec(memory_space=pltpu.VMEM)
    hbm = pl.BlockSpec(memory_space=pl.ANY)

    def buf(*shape):
        return pltpu.VMEM(shape, f32)

    def sem(*n):
        return pltpu.SemaphoreType.DMA(n)

    tile = (8, 128)
    bf16 = jnp.bfloat16
    scratch = [
        pltpu.SMEM((1,), f32), pltpu.SMEM((8,), f32), buf(128),
        buf(1, *tile), buf(1, *tile), buf(64, V), buf(64, 512), buf(512, 2048), buf(512, 2048),
        buf(4, 2, 64, 512), pltpu.VMEM((512, 512), bf16), pltpu.VMEM((512, 512), bf16), buf(4, 2, 64, V),
        buf(4, 2, 4, 4, *tile), buf(4, 8, 4, 16, V), pltpu.VMEM((2048, V), bf16), pltpu.VMEM((2048, V), bf16),
        buf(4, 2, 64, V), buf(4, 2, 64, V), buf(4, 2, 64, V), pltpu.VMEM((512, 3 * V), bf16),
        buf(1, 128), buf(32, 1, 128), buf(4, 2, 64, 128), buf(4, 2, 64, 128),
        buf(4, 2, 64, V), buf(4, 2, 64, V), buf(4, 2, 64, V),
        buf(4, 2, 4, 4, *tile), buf(3, 2, 4, 4, *tile), buf(3, 4, 2, 4, *tile), buf(4, 2, 4, *tile), buf(32, *tile),
        buf(16, 1, 128), buf(16, 1, 128), buf(16, 1, 256), buf(16, 1, 256), buf(1, 128), buf(1, 256), buf(2048, 128),
        sem(16), sem(22),
        sem(), sem(), sem(), sem(), sem(4), sem(8), sem(), sem(7), sem(7), sem(), sem(4), sem(), sem(),
        sem(2), sem(), sem(), sem(4),
    ]
    return pl.pallas_call(
        kernel,
        out_shape=(jax.ShapeDtypeStruct((1, 8, 128), f32), jax.ShapeDtypeStruct((1, 2), f32)),
        in_specs=[hbm] * 9,
        out_specs=(vmem, vmem),
        scratch_shapes=scratch,
        compiler_params=pltpu.CompilerParams(
            collective_id=0, has_side_effects=True, vmem_limit_bytes=60 * 1024 * 1024
        ),
        name="lanczos_step",
    )(beta, ev, q, prev, ec, pv, pc, w, b)


def solution(mesh):
    return jax.shard_map(
        per_device,
        mesh=mesh,
        in_specs=(
            P(None, "row", "col"),
            P(None, "row", "col"),
            P(),
            P("row"),
            P("col"),
            P(("row", "col"), None),
            P(("row", "col"), None),
            P("row", "col"),
            P("row", "col"),
        ),
        out_specs=(P(None, "row", "col"), P()),
        check_vma=False,
    )
```

time: 727 us -> 75.6 us (0.10)
  waiting for transfers between devices: 577 us -> 0 us
  blocking collectives: 85.2 us -> 0 us
  Pallas kernels: 0 us -> 71.8 us
  between operations: 19.6 us -> 1.29 us
  matrix products: 17 us -> 0 us
  local copies, waits for them, and re-layouts: 14.3 us -> 2.4 us
  starting transfers between devices: 9.62 us -> 0 us
    all_gather x2 -> x0, waiting for transfers between devices: 487 us -> none  [the longest x1 407 us: sent_together(): lax.all_gather(both, axis, axis=dim, tiled=True)]
    pallas_call x0 -> x1, Pallas kernels: none -> 71.8 us  [per_device(): pl.pallas_call(kernel, out_shape=(jax.ShapeDtypeStruct((1, 8, 128), f32),...]
    reduce_scatter x3 -> x0, waiting for transfers between devices: 67.8 us -> none  [reduced_to_own(): parts = lax.psum_scatter(parts, axes[k], scatter_dimension=0, tiled=True)]
    psum x5 -> x0, blocking collectives: 45.6 us -> none  [one_axis_at_a_time(): shard = lax.psum(shard, axis)]
    all_to_all x2 -> x0, blocking collectives: 39.6 us -> none  [the longest x1 27.3 us: sent_and_summed(): lax.all_to_all(parts, axis, split_axis=0, concat_axis=0, tiled=True)]
    all_to_all x2 -> x0, waiting for transfers between devices: 22.1 us -> none  [the longest x1 17.8 us: copy_for_each(): return lax.all_to_all(copies, axis, split_axis=0, concat_axis=0, tiled=True)]
    dot_general x7 -> x0, matrix products: 17 us -> none  [the longest x1 3.55 us: per_device(): jnp.einsum('mkv,nv->mkn', gather_directly(pair_local, COL, 0), panel, pre...]
    split x3 -> x0, local copies, waits for them, and re-layouts: 9.87 us -> none  [sent_together(): jnp.split(lax.all_gather(both, axis, axis=dim, tiled=True), ends, axis=al...]
  transfers between devices with their start and end apart: 7 -> 0, of which waited for: 7 -> 0; matrix products, arithmetic and copies ran while one was open for 0% -> 0% of each run, Pallas kernels for 0% -> 0%
where the time goes in v2:
time: 75.6 us; the launch traced here: 75.4 us
  Pallas kernels  71.8 us (95%)
  local copies, waits for them, and re-layouts  2.4 us (3%)
  between operations  1.29 us (2%)
    pallas_call x1, Pallas kernels, per_device(): pl.pallas_call(kernel, out_shape=(jax.ShapeDtypeStruct((1, 8, 128), f32),...  71.8 us
    unnamed x2, local copies, waits for them, and re-layouts  2.4 us

profile of v2, /device:TPU:1, one launch (start us, length us, event | category | flops | bytes accessed | tf_op | source)
XLA Modules:
  0.0 75.4 jit_solution(8392188844312690560)
XLA Ops:
  1.3 71.8 %lanczos_step.1 = (f32[1,8,128]{2,1,0:T(8,128)}, f32[1,2]{1,0:T(1,128)}) custom-call(f32[1]{0:T(128)S(6)} %copy.13.beta_hbm, f32[8]{0:T(128)} %ev_hbm.1, f32[1,8,128]{2,1,0:T(8,128)} %q_hbm.1, f32[1,8,128]{2,1,0:T(8,128)} %prev_hbm.1, f32[128]{0:T(128)} %ec_hbm.1, f32[64,256]{1,0:T(8,128)} %pv_hbm.1, f32[64,1024]{1,0:T(8,128)} %pc_hbm.1, f32[512,2048]{1,0:T(8,128)} %w_hbm.1, ...), custom_call_target="tpu_custom_call" | custom-call | tf_op jit(solution)/shard_map/lanczos_step/pallas_call | solution.py:550
  73.0 1.3 %copy.14 = f32[1,8,128]{2,1,0:T(8,128)} copy(f32[1,8,128]{2,1,0:T(8,128)} %get-tuple-element.4) | data formatting | bytes 8192
  74.3 1.1 %copy.15 = f32[1,2]{1,0:T(1,128)} copy(f32[1,2]{1,0:T(1,128)} %get-tuple-element.5) | data formatting | bytes 16

commit v3 on v2

v3 whole, which is shorter than its diff:
```python
import functools

import jax
import jax.numpy as jnp
from jax import lax
from jax.experimental import pallas as pl
from jax.experimental.pallas import tpu as pltpu
from jax.sharding import PartitionSpec as P

MESH = pl.DeviceIdType.MESH
HIGHEST = lax.Precision.HIGHEST
V, C = 256, 1024
EPS = 1e-06
NN = (((1,), (0,)), ((), ()))
NT = (((1,), (1,)), ((), ()))
TN = (((0,), (0,)), ((), ()))


def halves(a):
    hi = a.astype(jnp.bfloat16)
    return hi, (a - hi.astype(jnp.float32)).astype(jnp.bfloat16)


def left3(a, axis):
    hi, lo = halves(a)
    return jnp.concatenate([hi, lo, hi], axis=axis)


def right3(a, axis):
    hi, lo = halves(a)
    return jnp.concatenate([hi, hi, lo], axis=axis)


def dot(a, b, dims):
    return lax.dot_general(a, b, dims, preferred_element_type=jnp.float32)


def exact(a, b, dims):
    return lax.dot_general(a, b, dims, precision=HIGHEST, preferred_element_type=jnp.float32)


def kernel(
    beta_hbm, ev_hbm, q_hbm, prev_hbm, ec_hbm, pv_hbm, pc_hbm, w_hbm, b_hbm,
    out_ref,
    beta_ref, ev_ref, ec_ref, q_ref, prev_ref, own_pv, pc_other, w_ref, b_ref, pcr, pch, pcl, pv2, xg, pvc, ph, pl_,
    ap, ao, asum, aown, amps, dmine, dc, potx, pot0, ee, eo, dd, kb, r1a, r1b, acc1, r3,
    tz, txy, az, axy, mid, amid, dummy,
    load_sem, send_sem,
    x1r, x2r, x3r, p2r, p3r, p4r, cr, vr, ar_, a3r, dr, q0r, er, f1r, f3r, tr,
):
    row, col = lax.axis_index("row"), lax.axis_index("col")
    x, zhi, y = row // 8, (row // 4) % 2, row % 4
    zlo, core = col // 2, col % 2
    z = zhi * 4 + zlo
    other = 1 - core
    a, b = jnp.where(core == 0, y, x), jnp.where(core == 0, x, y)

    def dev(px, py, pz, pcore):
        return (px * 8 + (pz // 4) * 4 + py, (pz % 4) * 2 + pcore)

    def rc(src, dst, group, rs, to):
        return pltpu.make_async_remote_copy(
            src_ref=src, dst_ref=dst, send_sem=send_sem.at[group], recv_sem=rs, device_id=to, device_id_type=MESH
        )

    def px(d):
        return (x + d) % 4

    def py(d):
        return (y + d) % 4

    def pz(d):
        return (z + d) % 8

    def ab(da, db, dz=0):
        ja, jb = (a + da) % 4, (b + db) % 4
        return dev(jnp.where(core == 0, jb, ja), jnp.where(core == 0, ja, jb), pz(dz), core)

    partner = dev(x, y, z, other)

    def arrived(rs, kib):
        part = dummy.at[pl.ds(0, kib * 2)]
        rc(part, part, 0, rs, partner).wait_recv()

    def left(group, kib):
        part = dummy.at[pl.ds(0, kib * 2)]
        rc(part, part, group, x1r, partner).wait_send()

    def rows_arrived(rs, ref, n):
        part = ref.at[pl.ds(0, n)]
        rc(part, part, 0, rs, partner).wait_recv()

    def rows_left(group, ref, n):
        part = ref.at[pl.ds(0, n)]
        rc(part, part, group, x1r, partner).wait_send()

    lanes = [slice(c * 128, (c + 1) * 128) for c in range(4)]
    pairs = [(q_hbm, q_ref), (pv_hbm, own_pv)]
    for c in range(4):
        mine, its = (pl.ds(pl.multiple_of((c * 2 + k) * 128, 128), 128) for k in (core, other))
        pairs.append((pc_hbm.at[:, mine], pcr.at[zlo, core, :, lanes[c]]))
        pairs.append((pc_hbm.at[:, its], pc_other.at[:, lanes[c]]))
    pairs += [(prev_hbm, prev_ref), (ec_hbm, ec_ref), (ev_hbm, ev_ref), (beta_hbm, beta_ref)]
    pairs += [(w_hbm, w_ref), (b_hbm, b_ref)]
    loads = [pltpu.make_async_copy(s, d, load_sem.at[i]) for i, (s, d) in enumerate(pairs)]
    for c in loads:
        c.start()

    barrier = pltpu.get_barrier_semaphore()

    def greet(to):
        pl.semaphore_signal(barrier, inc=1, device_id=to, device_id_type=MESH)

    in_own_block = (x == zlo) & (core == zhi)
    own_unit = (x == 0) & (zlo == 0) & (core == zhi)
    for c in range(2):
        to = dev(zlo, y, core * 4 + (x - zlo + 4) % 4, (core + c) % 2)
        if c == 0:
            pl.when(jnp.logical_not(own_unit))(functools.partial(greet, to))
        else:
            greet(to)
    for d in range(1, 4):
        greet(dev(px(d), y, z, core))
        greet(dev(x, py(d), z, core))
    for d in (4, 3, 5, 2, 6, 1, 7):
        greet(dev(x, y, pz(d), core))
        greet(dev(x, y, pz(d), other))
    greet(partner)
    loads[0].wait()
    xg[x, zhi, y, zlo] = q_ref[0]
    for i in range(1, 10):
        loads[i].wait()

    @pl.when(own_unit)
    def _():
        pvc[y, zlo, core] = own_pv[...]
        pl.semaphore_wait(barrier, 21 + 1)

    @pl.when(jnp.logical_not(own_unit))
    def _():
        pl.semaphore_wait(barrier, 21 + 2)

    for d in (4, 3, 5, 2, 6, 1, 7):
        rc(q_ref.at[0], xg.at[x, zhi, y, zlo], 0, x1r, dev(x, y, pz(d), core)).start()

    for i in range(2):
        copy = rc(own_pv, pvc.at[y, zlo, core], 2, p2r, dev((x + zlo) % 4, y, x + 4 * ((zhi + i) % 2), zhi))
        if i == 0:
            pl.when(jnp.logical_not(own_unit))(copy.start)
        else:
            copy.start()

    def inside(s):
        return (zlo + s >= 0) & (zlo + s < 4)

    own_rows = pcr.at[zlo, core]
    rc(pc_other, own_rows, 1, cr.at[3, 1], partner).start()
    rc(own_pv, pv2.at[core], 2, vr, partner).start()
    pv2[core] = own_pv[...]
    def rows_came(s, kind):
        part = pcr.at[zlo - s, core if kind == 0 else other]
        rc(part, part, 3, cr.at[s + 3, kind], partner).wait_recv()

    arrived(x1r, 28)

    part = xg.at[x, :, y]
    for d in (2, 1, 3):
        rc(part, part, 0, x2r, ab(d, 0)).start()

    def two(wait, sem, extra=0):
        @pl.when(own_unit)
        def _():
            wait(sem, 64 + extra)

        @pl.when(jnp.logical_not(own_unit))
        def _():
            wait(sem, 128 + extra)

    two(arrived, p2r)

    def place(ja, jb):
        return jnp.where(core == 0, ja, jb), (jnp.where(core == 0, jb, ja) - zlo + 4) % 4

    def unit(da, db):
        return pvc.at[place((a + da) % 4, (b + db) % 4)]

    def p3(d):
        return rc(unit(0, 0), unit(0, 0), 5, p3r.at[d], ab(d, 0))

    def p4(d, rel):
        return rc(unit(rel, 0), unit(rel, 0), 7 if d == 2 else 6, p4r.at[d], ab(0, d))

    for d in (2, 1, 3):
        p3(d).start()
    for d in (1, 3, 2):
        p4(d, 0).start()
    for s in (1, -1):

        @pl.when(inside(s))
        def _():
            rc(own_rows, own_rows, 3, cr.at[s + 3, 0], (row, (zlo + s) * 2 + core)).start()
            rc(pc_other, own_rows, 3, cr.at[s + 3, 1], (row, (zlo + s) * 2 + other)).start()

    arrived(x2r, 96)

    def chunk(c, d):
        return xg.at[px(d)] if c == 0 else xg.at[:, :, py(d)]

    for c in range(2):

        @pl.when(core == c)
        def _():
            for d in (2, 1, 3):
                rc(chunk(c, 0), chunk(c, 0), 8, x3r, ab(0, d)).start()

    for d in (1, 3, 2):
        part = unit(4 - d, 0)
        rc(part, part, 5, p3r.at[d], partner).wait_recv()
        p4(1, 4 - d).start()
        p4(3, 4 - d).start()
    for rel in (3, 1, 2):
        p4(2, rel).start()

    def take_rows(s):
        step = 1 if s > 0 else -1

        @pl.when(inside(-s))
        def _():
            for kind in range(2):
                rows_came(s, kind)

                if abs(s) < 3:

                    @pl.when(inside(step))
                    def _():
                        part = pcr.at[zlo - s, core if kind == 0 else other]
                        rc(part, part, 9, cr.at[s + step + 3, kind], (row, (zlo + step) * 2 + core)).start()

    take_rows(1)
    take_rows(-1)
    arrived(x3r, 384)
    rows_came(0, 1)

    xs = left3(jnp.concatenate([xg[:, :, :, c].reshape(V, 128) for c in range(4)], axis=1), 1)

    def a1(zl):
        return rc(ap.at[zl], ao.at[zl], 10, ar_.at[zl], partner)

    def amp_of(zl):
        at = pl.ds(pl.multiple_of(zl * 128, 128), 128)
        hi, lo = halves(pcr[zl].reshape(128, 512))
        pch[at] = hi
        pcl[at] = lo
        ap[zl] = dot(jnp.concatenate([hi, hi, lo], axis=1), xs, NT).reshape(2, 64, V)
        a1(zl).start()

    amp_of(zlo)

    for s in (1, -1):
        pl.when(inside(-s))(functools.partial(amp_of, zlo - s))

    a1(zlo).wait_recv()
    asum[zlo] = ap[zlo] + ao[zlo]
    own_amp = asum[zlo]
    arrived(vr, 64)
    dens = (pv2[...] * own_amp).reshape(128, V)
    dmine[...] = exact(jnp.ones((8, V), jnp.float32), dens, NT)[0:1]
    at_end = (zlo == 0) | (zlo == 3)

    @pl.when(at_end)
    def _():
        aown[...] = asum[zlo, core]
        for c in (core, other):
            rc(aown, asum.at[zlo, core], 1, a3r, (row, (3 - zlo) * 2 + c)).start()

    slot = y * 4 + zlo
    own_row = in_own_block & (core == 0)

    def density_to(dx, dy, h):
        to = dev(px(dx), py(dy), x + 4 * ((zhi + h) % 2), zhi)
        rc(dmine, dc.at[slot], 11, dr, to).start()

    @pl.when(core == 1)
    def _():
        for i in range(24):
            density_to((2, 1, 3)[i // 8], (i // 2 + 2) % 4, i % 2)

    @pl.when(core == 0)
    def _():
        for i in range(7):
            density_to(0, (2, 2, 1, 1, 3, 3, 0)[i], (0, 1, 0, 1, 0, 1, 1)[i])

        @pl.when(own_row)
        def _():
            dc[slot] = dmine[...]

        pl.when(jnp.logical_not(own_row))(functools.partial(density_to, 0, 0, 0))

    take_rows(2)
    take_rows(-2)
    for s in (2, -2):
        pl.when(inside(-s))(functools.partial(amp_of, zlo - s))

    near = zlo // 2
    far = 1 - near

    def use(zl):
        amps[pl.ds(pl.multiple_of(zl * 128, 128), 128)] = left3(asum[zl].reshape(128, V), 1)

    def join(zl):
        a1(zl).wait_recv()
        asum[zl] = ap[zl] + ao[zl]
        use(zl)

    use(zlo)
    join(near * 2 + 1 - zlo % 2)

    loads[14].wait()

    def split(d):
        hi, lo = halves(jnp.concatenate([pvc[place(j, (b + d) % 4)].reshape(128, V) for j in range(4)], axis=0))
        ph[d] = hi
        pl_[d] = lo

    def block(d, pair):
        hi, lo = ph[d], pl_[d]
        rows = pl.ds(pl.multiple_of(pair * 256, 256), 256)
        spots = [place(j, (b + d) % 4) for j in range(4)]
        columns = [pl.ds(pl.multiple_of(ys * 512 + zs * 128, 128), 128) for ys, zs in spots]
        weights = jnp.concatenate([w_ref[rows, at] for at in columns], axis=1)
        terms = dot(amps[rows], jnp.concatenate([hi, hi, lo], axis=1), NT) * weights
        return dot(left3(terms, 1), jnp.concatenate([hi, hi, lo], axis=0), NN)

    def e1(i, pair):
        part = pl.ds(2 * pair, 2)
        return rc(ee.at[part], eo.at[part], 13, er.at[i], partner)

    split(0)
    part = block(0, near)
    arrived(p4r.at[1], 512)
    split(3)
    part = part + block(3, near)
    arrived(p4r.at[3], 512)
    split(1)
    part = part + block(1, near)
    ee[pl.ds(2 * near, 2)] = part.reshape(2, 2, 64, V)
    arrived(p4r.at[2], 512)
    split(2)
    ee[pl.ds(2 * near, 2)] += block(2, near).reshape(2, 2, 64, V)
    e1(0, near).start()

    loads[15].wait()

    @pl.when(own_row)
    def _():
        rows_arrived(dr, dc, 15)

    @pl.when(jnp.logical_not(own_row))
    def _():
        rows_arrived(dr, dc, 16)

    pot = None
    for t in range(16):
        piece = b_ref[:, t * 128 : (t + 1) * 128] * dc[t]
        pot = piece if pot is None else pot + piece
    pot = jnp.sum(pot, axis=1, keepdims=True)
    diag = lax.broadcasted_iota(jnp.int32, (128, 128), 0) == lax.broadcasted_iota(jnp.int32, (128, 128), 1)
    for j in range(4):
        potx[j] = jnp.sum(jnp.where(diag, pot[j * 128 : (j + 1) * 128], 0.0), axis=0, keepdims=True)
    for d in (2, 1, 3, 0):
        zl = (zlo + d) % 4
        for c in range(2):
            if d or c:
                rc(potx.at[zl], pot0.at[2 * d + c], 15, q0r, (row, zl * 2 + (core + c) % 2)).start()
    pot0[0] = potx[zlo]
    for s in (2, -2):
        pl.when(inside(-s))(functools.partial(join, zlo - s))

    @pl.when(at_end)
    def _():
        arrived(a3r, 128)
        use(3 - zlo)

    @pl.when(jnp.logical_not(at_end))
    def _():
        join(3 - zlo)

    part = block(0, far) + block(3, far) + block(1, far) + block(2, far)
    ee[pl.ds(2 * far, 2)] = part.reshape(2, 2, 64, V)
    e1(1, far).start()

    for s in (3, -3):
        take_rows(s)

        @pl.when(inside(-s))
        def _():
            at = pl.ds(pl.multiple_of((zlo - s) * 128, 128), 128)
            hi, lo = halves(pcr[zlo - s].reshape(128, 512))
            pch[at] = hi
            pcl[at] = lo

    def kpart(i, pair):
        e1(i, pair).wait_recv()
        at = pl.ds(2 * pair, 2)
        both = -(ee[at] + eo[at])
        dd[at] = both
        rows = pl.ds(pl.multiple_of(pair * 256, 256), 256)
        hi, lo = pch[rows], pcl[rows]
        return dot(left3(both.reshape(256, V), 0), jnp.concatenate([hi, hi, lo], axis=0), TN)

    kfull = kpart(0, near)
    kfull = kfull + kpart(1, far)
    rows_arrived(q0r, pot0, 7)
    pot_row = jnp.sum(pot0[...], axis=0)
    pot2 = 2.0 * jnp.sum(jnp.where(diag, pot_row, 0.0), axis=1, keepdims=True)
    bare = pot2 * pv2[...].reshape(128, V)
    rows = pl.ds(pl.multiple_of(zlo * 128, 128), 128)
    hi, lo = pch[rows], pcl[rows]
    kfull = kfull + dot(left3(bare, 0), jnp.concatenate([hi, hi, lo], axis=0), TN)
    dd[zlo] = dd[zlo] + bare.reshape(2, 64, V)
    for c in range(4):
        kb[:, :, :, c] = kfull[:, lanes[c]].reshape(4, 2, 4, 8, 128)

    for c in range(2):

        @pl.when(core == c)
        def _():
            for d in (2, 1, 3):
                part = kb.at[px(d)] if c == 0 else kb.at[:, :, py(d)]
                rc(part, (r1a if c == 0 else r1b).at[d - 1], 16, f1r, ab(0, d)).start()

    for i in (10, 11, 12, 13):
        loads[i].wait()
    q, prev = q_ref[0], prev_ref[0]
    sub8 = lax.broadcasted_iota(jnp.int32, (8, 128), 0)
    ev = jnp.zeros((8, 128), jnp.float32)
    for i in range(8):
        ev = jnp.where(sub8 == i, ev_ref[i], ev)
    gaps = ec_ref[...].reshape(1, 128) - ev
    prod = (dd[:, core] * asum[:, core]).reshape(256, V)
    prod = jnp.sum(prod[:, 0:128] + prod[:, 128:256], axis=0, keepdims=True)
    qq = jnp.sum(q * q, axis=0, keepdims=True)
    qu = prod + jnp.sum(gaps * q * q, axis=0, keepdims=True)
    az[0] = jnp.concatenate([qu, qq], axis=1)

    def t1(src, dst, group, rs):
        for d in (4, 3, 5, 2, 6, 1, 7, 0):
            for j in (d, d + 8):
                if j:
                    to = dev(x, y, pz(d), core if j < 8 else other)
                    rc(src, dst.at[j], group, rs, to).start()

    def t2(src, dst, group, rs):
        for j in (10, 9, 11, 6, 14, 2, 8, 5, 7, 13, 15, 1, 3, 4, 12):
            rc(src, dst.at[j], group, rs, dev(px(j // 4), py(j % 4), z, core)).start()

    t1(az.at[0], az, 18, tr.at[0])

    arrived(f1r, 384)
    for c in range(2):

        @pl.when(core == c)
        def _():
            if c == 0:
                for i in range(2):
                    acc1[:, i] = kb[x, i] + r1a[0, i] + r1a[1, i] + r1a[2, i]
            else:
                acc1[...] = kb[:, :, y] + r1b[0] + r1b[1] + r1b[2]

    for da in (2, 1, 3, 0):
        for dz in (4, 3, 5, 2, 6, 1, 7, 0):
            if da or dz:
                zz = pz(dz)
                part = acc1.at[(a + da) % 4, zz // 4, zz % 4]
                rc(part, r3.at[da * 8 + dz], 17, f3r, ab(da, 0, dz)).start()
    rows_arrived(tr.at[0], az, 15)
    amid[...] = jnp.sum(az[...], axis=0)
    axy[0] = amid[...]
    t2(amid, axy, 19, tr.at[1])
    arrived(f3r, 124)
    tile = acc1[a, zhi, zlo] + jnp.sum(r3[1:32], axis=0)
    inv = 1.0 / (V * C)
    bp = beta_ref[...]
    rows_arrived(tr.at[1], axy, 15)
    total = jnp.sum(axy[...], axis=0)
    qu = jnp.sum(total[:, 0:128], axis=1, keepdims=True)
    qq = jnp.sum(total[:, 128:256], axis=1, keepdims=True)
    alpha = qu * inv / (qq * inv + EPS)
    resid = tile + (gaps - alpha) * q - bp * prev
    tz[0] = jnp.sum(resid * resid, axis=0, keepdims=True)
    t1(tz.at[0], tz, 20, tr.at[2])
    rows_arrived(tr.at[2], tz, 15)
    mid[...] = jnp.sum(tz[...], axis=0)
    t2(mid, txy, 21, tr.at[3])
    txy[0] = mid[...]
    rows_arrived(tr.at[3], txy, 15)
    ww = jnp.sum(jnp.sum(txy[...], axis=0), axis=1, keepdims=True)
    beta = jnp.sqrt(ww * inv + EPS)
    out_ref[0:8] = resid / beta
    out_ref[8:16] = jnp.where(lax.broadcasted_iota(jnp.int32, (8, 128), 1) == 0, alpha, beta)

    left(0, 124)
    two(left, 2, 64)
    left(5, 384)
    left(6, 1024)
    left(7, 512)
    left(8, 384)

    @pl.when((zlo == 0) | (zlo == 3))
    def _():
        left(1, 256)
        left(3, 256)
        left(10, 384)

    @pl.when((zlo == 1) | (zlo == 2))
    def _():
        left(1, 128)
        left(3, 512)
        left(9, 768)
        left(10, 512)


    @pl.when(core == 1)
    def _():
        left(11, 12)

    @pl.when(core == 0)
    def _():
        pl.when(own_row)(lambda: rows_left(11, dc, 7))
        pl.when(jnp.logical_not(own_row))(lambda: rows_left(11, dc, 8))

    left(13, 512)
    rows_left(15, pot0, 7)
    left(16, 384)
    left(17, 124)
    rows_left(18, az, 15)
    rows_left(19, axy, 15)
    rows_left(20, tz, 15)
    rows_left(21, txy, 15)


def split_results(both_ref, out_ref, coef_ref):
    out_ref[0] = both_ref[0:8]
    coef_ref[...] = both_ref[8:9, 0:2]


def per_device(q, prev, beta, ev, ec, pv, pc, w, b):
    f32 = jnp.float32
    vmem = pl.BlockSpec(memory_space=pltpu.VMEM)
    hbm = pl.BlockSpec(memory_space=pltpu.HBM)

    def buf(*shape):
        return pltpu.VMEM(shape, f32)

    def sem(*n):
        return pltpu.SemaphoreType.DMA(n)

    tile = (8, 128)
    bf16 = jnp.bfloat16
    scratch = [
        buf(1, 1), pltpu.SMEM((8,), f32), buf(128),
        buf(1, *tile), buf(1, *tile), buf(64, V), buf(64, 512), buf(512, 2048), buf(512, 2048),
        buf(4, 2, 64, 512), pltpu.VMEM((512, 512), bf16), pltpu.VMEM((512, 512), bf16), buf(2, 64, V),
        buf(4, 2, 4, 4, *tile), buf(4, 4, 2, 64, V), pltpu.VMEM((4, 512, V), bf16), pltpu.VMEM((4, 512, V), bf16),
        buf(4, 2, 64, V), buf(4, 2, 64, V), buf(4, 2, 64, V), buf(64, V), pltpu.VMEM((512, 3 * V), bf16),
        buf(1, 128), buf(16, 1, 128), buf(4, 1, 128), buf(8, 1, 128),
        buf(4, 2, 64, V), buf(4, 2, 64, V), buf(4, 2, 64, V),
        buf(4, 2, 4, 4, *tile), buf(3, 2, 4, 4, *tile), buf(3, 4, 2, 4, *tile), buf(4, 2, 4, *tile), buf(32, *tile),
        buf(16, 1, 128), buf(16, 1, 128), buf(16, 1, 256), buf(16, 1, 256), buf(1, 128), buf(1, 256), buf(2048, 128),
        sem(16), sem(22),
        sem(), sem(), sem(), sem(), sem(4), sem(4), sem(7, 2), sem(), sem(4), sem(), sem(), sem(),
        sem(2), sem(), sem(), sem(4),
    ]
    both = pl.pallas_call(
        kernel,
        out_shape=jax.ShapeDtypeStruct((16, 128), f32),
        in_specs=[hbm] * 9,
        out_specs=vmem,
        scratch_shapes=scratch,
        compiler_params=pltpu.CompilerParams(
            collective_id=0, has_side_effects=True, vmem_limit_bytes=60 * 1024 * 1024
        ),
        name="lanczos_step",
    )(beta.reshape(1, 1), ev, q, prev, ec, pv, pc, w, b)
    return pl.pallas_call(
        split_results,
        out_shape=(jax.ShapeDtypeStruct((1, 8, 128), f32), jax.ShapeDtypeStruct((1, 2), f32)),
        in_specs=[vmem],
        out_specs=(vmem, vmem),
        name="split_results",
    )(both)


def solution(mesh):
    return jax.shard_map(
        per_device,
        mesh=mesh,
        in_specs=(
            P(None, "row", "col"),
            P(None, "row", "col"),
            P(),
            P("row"),
            P("col"),
            P(("row", "col"), None),
            P(("row", "col"), None),
            P("row", "col"),
            P("row", "col"),
        ),
        out_specs=(P(None, "row", "col"), P()),
        check_vma=False,
    )
```

time: 75.6 us -> 72.7 us (0.962)
  local copies, waits for them, and re-layouts: 2.4 us -> 0 us
    unnamed x2 -> x0, local copies, waits for them, and re-layouts: 2.4 us -> none
    pallas_call x1 -> x2, Pallas kernels: 71.8 us -> 71.2 us  [the longest x1 69.9 us: per_device(): pl.pallas_call(kernel, out_shape=jax.ShapeDtypeStruct((16, 128), f32), in...]
where the time goes in v3:
time: 72.7 us; the launch traced here: 72.5 us
  Pallas kernels  71.2 us (98%)
  between operations  1.29 us (2%)
    pallas_call x1, Pallas kernels, per_device(): pl.pallas_call(kernel, out_shape=jax.ShapeDtypeStruct((16, 128), f32), in...  69.9 us

profile of v3, /device:TPU:1, one launch (start us, length us, event | category | flops | bytes accessed | tf_op | source)
XLA Modules:
  0.0 72.5 jit_solution(7452741179408162917)
XLA Ops:
  1.3 69.9 %lanczos_step.1.both_ref = f32[16,128]{1,0:T(8,128)} custom-call(f32[1,1]{1,0:T(1,128)} %bitcast.1.beta_hbm, f32[8]{0:T(128)} %ev_hbm.1, f32[1,8,128]{2,1,0:T(8,128)} %q_hbm.1, f32[1,8,128]{2,1,0:T(8,128)} %prev_hbm.1, f32[128]{0:T(128)} %ec_hbm.1, f32[64,256]{1,0:T(8,128)} %pv_hbm.1, f32[64,1024]{1,0:T(8,128)} %pc_hbm.1, f32[512,2048]{1,0:T(8,128)} %w_hbm.1, ...), custom_call_target="tpu_custom_call" | custom-call | tf_op jit(solution)/shard_map/lanczos_step/pallas_call | solution.py:574
  71.2 1.3 %split_results.1 = (f32[1,8,128]{2,1,0:T(8,128)}, f32[1,2]{1,0:T(1,128)}) custom-call(f32[16,128]{1,0:T(8,128)} %lanczos_step.1.both_ref), custom_call_target="tpu_custom_call" | custom-call | tf_op jit(solution)/shard_map/split_results/pallas_call | solution.py:585

commit v4 on v3

--- a/solution.py
+++ b/solution.py
@@ -192,8 +192,6 @@
 
     for d in (2, 1, 3):
         p3(d).start()
-    for d in (1, 3, 2):
-        p4(d, 0).start()
     for s in (1, -1):
 
         @pl.when(inside(s))
@@ -212,14 +210,6 @@
         def _():
             for d in (2, 1, 3):
                 rc(chunk(c, 0), chunk(c, 0), 8, x3r, ab(0, d)).start()
-
-    for d in (1, 3, 2):
-        part = unit(4 - d, 0)
-        rc(part, part, 5, p3r.at[d], partner).wait_recv()
-        p4(1, 4 - d).start()
-        p4(3, 4 - d).start()
-    for rel in (3, 1, 2):
-        p4(2, rel).start()
 
     def take_rows(s):
         step = 1 if s > 0 else -1
@@ -236,8 +226,22 @@
                         part = pcr.at[zlo - s, core if kind == 0 else other]
                         rc(part, part, 9, cr.at[s + step + 3, kind], (row, (zlo + step) * 2 + core)).start()
 
+    def pass_units():
+        for d in (1, 3, 2):
+            part = unit(4 - d, 0)
+            rc(part, part, 5, p3r.at[d], partner).wait_recv()
+            p4(1, 4 - d).start()
+            p4(3, 4 - d).start()
+        for rel in (3, 1, 2):
+            p4(2, rel).start()
+
+    for d in (1, 3, 2):
+        p4(d, 0).start()
+
+    pl.when(core == 1)(pass_units)
     take_rows(1)
     take_rows(-1)
+    pl.when(core == 0)(pass_units)
     arrived(x3r, 384)
     rows_came(0, 1)
 
@@ -295,11 +299,6 @@
             dc[slot] = dmine[...]
 
         pl.when(jnp.logical_not(own_row))(functools.partial(density_to, 0, 0, 0))
-
-    take_rows(2)
-    take_rows(-2)
-    for s in (2, -2):
-        pl.when(inside(-s))(functools.partial(amp_of, zlo - s))
 
     near = zlo // 2
     far = 1 - near
@@ -337,6 +336,11 @@
 
     split(0)
     part = block(0, near)
+    take_rows(2)
+    take_rows(-2)
+    for s in (2, -2):
+        pl.when(inside(-s))(functools.partial(amp_of, zlo - s))
+
     arrived(p4r.at[1], 512)
     split(3)
     part = part + block(3, near)

time: 72.7 us -> 71.7 us (0.986)
  Pallas kernels: 71.2 us -> 70.2 us
    pallas_call x1, Pallas kernels: 69.9 us -> 68.9 us  [per_device(): pl.pallas_call(kernel, out_shape=jax.ShapeDtypeStruct((16, 128), f32), in...]
where the time goes in v4:
time: 71.7 us; the launch traced here: 71.5 us
  Pallas kernels  70.2 us (98%)
  between operations  1.29 us (2%)
    pallas_call x1, Pallas kernels, per_device(): pl.pallas_call(kernel, out_shape=jax.ShapeDtypeStruct((16, 128), f32), in...  68.9 us

profile of v4, /device:TPU:1, one launch (start us, length us, event | category | flops | bytes accessed | tf_op | source)
XLA Modules:
  0.0 71.5 jit_solution(15881922852297974976)
XLA Ops:
  1.3 68.9 %lanczos_step.1.both_ref = f32[16,128]{1,0:T(8,128)} custom-call(f32[1,1]{1,0:T(1,128)} %bitcast.1.beta_hbm, f32[8]{0:T(128)} %ev_hbm.1, f32[1,8,128]{2,1,0:T(8,128)} %q_hbm.1, f32[1,8,128]{2,1,0:T(8,128)} %prev_hbm.1, f32[128]{0:T(128)} %ec_hbm.1, f32[64,256]{1,0:T(8,128)} %pv_hbm.1, f32[64,1024]{1,0:T(8,128)} %pc_hbm.1, f32[512,2048]{1,0:T(8,128)} %w_hbm.1, ...), custom_call_target="tpu_custom_call" | custom-call | tf_op jit(solution)/shard_map/lanczos_step/pallas_call | solution.py:578
  70.2 1.3 %split_results.1 = (f32[1,8,128]{2,1,0:T(8,128)}, f32[1,2]{1,0:T(1,128)}) custom-call(f32[16,128]{1,0:T(8,128)} %lanczos_step.1.both_ref), custom_call_target="tpu_custom_call" | custom-call | tf_op jit(solution)/shard_map/split_results/pallas_call | solution.py:589

commit v5 on v4

--- a/solution.py
+++ b/solution.py
@@ -190,7 +190,7 @@
     def p4(d, rel):
         return rc(unit(rel, 0), unit(rel, 0), 7 if d == 2 else 6, p4r.at[d], ab(0, d))
 
-    for d in (2, 1, 3):
+    for d in (1, 3):
         p3(d).start()
     for s in (1, -1):
 
@@ -235,6 +235,7 @@
         for rel in (3, 1, 2):
             p4(2, rel).start()
 
+    p3(2).start()
     for d in (1, 3, 2):
         p4(d, 0).start()
 

time: 71.7 us -> 71.3 us (level)
  no operation moved by 1% of the time
where the time goes in v5:
time: 71.3 us; the launch traced here: 71.1 us
  Pallas kernels  69.9 us (98%)
  between operations  1.29 us (2%)
    pallas_call x1, Pallas kernels, per_device(): pl.pallas_call(kernel, out_shape=jax.ShapeDtypeStruct((16, 128), f32), in...  68.6 us

profile of v5, /device:TPU:1, one launch (start us, length us, event | category | flops | bytes accessed | tf_op | source)
XLA Modules:
  0.0 71.1 jit_solution(4766072528430316100)
XLA Ops:
  1.3 68.6 %lanczos_step.1.both_ref = f32[16,128]{1,0:T(8,128)} custom-call(f32[1,1]{1,0:T(1,128)} %bitcast.1.beta_hbm, f32[8]{0:T(128)} %ev_hbm.1, f32[1,8,128]{2,1,0:T(8,128)} %q_hbm.1, f32[1,8,128]{2,1,0:T(8,128)} %prev_hbm.1, f32[128]{0:T(128)} %ec_hbm.1, f32[64,256]{1,0:T(8,128)} %pv_hbm.1, f32[64,1024]{1,0:T(8,128)} %pc_hbm.1, f32[512,2048]{1,0:T(8,128)} %w_hbm.1, ...), custom_call_target="tpu_custom_call" | custom-call | tf_op jit(solution)/shard_map/lanczos_step/pallas_call | solution.py:579
  69.8 1.3 %split_results.1 = (f32[1,8,128]{2,1,0:T(8,128)}, f32[1,2]{1,0:T(1,128)}) custom-call(f32[16,128]{1,0:T(8,128)} %lanczos_step.1.both_ref), custom_call_target="tpu_custom_call" | custom-call | tf_op jit(solution)/shard_map/split_results/pallas_call | solution.py:590
